TPU v7x, 32 devices: a whole 2x2x4 slice. The times are simulated.
32 devices in a mesh: mat: 4 (over x, core), frac: 8 (over z, y).
Axes of the slice: x: 2, y: 2, z: 4, core: 2. Of those that a mesh axis runs over, the one named last changes fastest.
Arguments:
- pressure_start: float32 [64, 512, 256], P('mat', 'frac'), may hold values from -6 to 6
- face_trans: float32 [3, 64, 512, 256], P(None, 'mat', 'frac'), may hold values from 0.2 to 2
- cell_coef: float32 [64, 512, 256], P('mat', 'frac'), may hold values from 0.05 to 0.5
- matrix_source: float32 [64, 512, 256], P('mat', 'frac'), may hold values from -6 to 6
- mortar_owner: int32 [16384, 1], P(('mat', 'frac')), may hold values from 0 to 31; in each aligned block of 512 rows (0 to 511, 512 to 1023, ...) at most 32 rows name the same one
- mortar_cell: int32 [16384], P(('mat', 'frac')), may hold values from 0 to 262143
- mortar_frac: int32 [16384], P(('mat', 'frac')), may hold values from 0 to 8191
- mortar_kappa: float32 [16384], P(('mat', 'frac')), may hold values from 0.5 to 2
- tiles: float32 [64, 4, 128, 128], P('frac'), may hold values from -0.25 to 0.25
- tile_cols: int32 [64, 4], P('frac'), may hold values from 0 to 63
- frac_diag: float32 [8192], P('frac'), may hold values from 4 to 8
- frac_source: float32 [8192], P('frac'), may hold values from -6 to 6
- fracture_start: float32 [8192], P('frac'), may hold values from -6 to 6
Outputs:
- pressure: float32 [64, 512, 256], P('mat', 'frac')
- fracture: float32 [8192], P('frac')
- flux: float32 [16384], P(('mat', 'frac'))
Inputs may be any that keep to these rules, and one draw needn't show every extreme that they name: `mortar_owner`: among the 512 mortar cells of one device, at most 32 name the same owner, and in some devices some owner is named exactly 32 times.
All inputs are finite; a program needn't handle non-finite values.
Results may differ from a plain program's by a relative error of at most 0.00015.
Values sent between devices are 32-bit elements; how exact they have to be, the bound alone decides.
A program may use at most 128 MiB of HBM per device.

v0:
```python
import functools

import jax
import jax.numpy as jnp
from jax import lax
from jax.experimental import pallas as pl
from jax.experimental.pallas import tpu as pltpu
from jax.sharding import PartitionSpec as P

SWEEPS = 2
CG_ITERS = 3
OUTER = 2

EXACT = lax.Precision.HIGHEST
MESH = pl.DeviceIdType.MESH

relax_weight = 0.8


def coupled_kernel(n_frac, n_mat, *refs):
    (press_ref, face_ref, cell_ref, msource_ref, where_ref, kappa_ref, place_ref, tiles_ref, cols_ref, cols_row_ref,
     diag_ref, begin_ref, fsource_ref, out_ref, own_ref, flux_ref, *scratch) = refs
    (gather_ref, outgo_ref, income_ref, mat_ref, back_ref, forth_ref, grid_ref, tx_ref, inv_ref, base_ref, row_hot_ref,
     lane_hot_ref, side_ref, edge_ref, ty_edge_ref, ty_side_ref, gather_send, gather_recv, part_send, part_recv,
     mat_send, mat_recv, halo_send, halo_recv) = scratch
    rows, tiles_row = tiles_ref.shape[0], tiles_ref.shape[1]
    size_b = tiles_ref.shape[3]
    width_x, width_y, depth_z = press_ref.shape
    slots = place_ref.shape[1]
    blocks = rows * n_frac
    sweeps = OUTER * SWEEPS
    phases = CG_ITERS + 1
    me = lax.axis_index("frac")
    me_mat = lax.axis_index("mat")
    mine = pl.ds(pl.multiple_of(me * rows, rows), rows)

    barrier = pltpu.get_barrier_semaphore()
    for k in range(1, n_frac):
        pl.semaphore_signal(barrier, inc=1, device_id={"frac": lax.rem(me + k, n_frac)}, device_id_type=MESH)
    for k in range(1, n_mat):
        pl.semaphore_signal(barrier, inc=1, device_id={"mat": lax.rem(me_mat + k, n_mat)}, device_id_type=MESH)
    pl.semaphore_wait(barrier, n_frac + n_mat - 2)

    sent = []
    pieces = []

    def fill(count):
        for _ in range(min(count, len(pieces))):
            pieces.pop(0)()

    def send(src, dst, send_sem, recv_sem, device):
        copy = pltpu.make_async_remote_copy(
            src_ref=src, dst_ref=dst, send_sem=send_sem, recv_sem=recv_sem, device_id=device, device_id_type=MESH
        )
        copy.start()
        sent.append(copy)
        return copy

    def gather(phase, value):
        gather_ref[phase, mine, :] = value
        here = gather_ref.at[phase, mine]
        return [
            send(here, here, gather_send.at[phase, k - 1], gather_recv.at[phase, k - 1], {"frac": lax.rem(me + k, n_frac)})
            for k in range(1, n_frac)
        ]

    def exchange(phase, low, high, count):
        part = pl.ds(low, high - low)
        copies = []
        for k in range(1, n_frac):
            target = lax.rem(me + k, n_frac)
            copies.append(
                send(
                    outgo_ref.at[phase, target, part],
                    income_ref.at[phase, me, part],
                    part_send.at[phase, k - 1],
                    part_recv.at[phase, k - 1],
                    {"frac": target},
                )
            )
        income_ref[phase, me, part, :] = outgo_ref[phase, me, part, :]
        fill(count)
        for copy in copies:
            copy.wait_recv()
        total = income_ref[phase, 0, part, :]
        for k in range(1, n_frac):
            total = total + income_ref[phase, k, part, :]
        return total

    def products(phase, with_back):
        def row(r, carry):
            across = gather_ref[phase, pl.ds(me * rows + r, 1), :]
            down = jnp.broadcast_to(across, (size_b, size_b)).T
            total = jnp.zeros((size_b, size_b), jnp.float32)
            for t in range(tiles_row):
                tile = tiles_ref[r, t]
                total = total + tile * gather_ref[phase, pl.ds(cols_ref[r, t], 1), :]
                if with_back:
                    back_ref[pl.ds(r * tiles_row + t, 1), :] = jnp.sum(tile * down, axis=0, keepdims=True)
            forth_ref[pl.ds(r, 1), :] = jnp.sum(total.T, axis=0, keepdims=True)
            return carry

        lax.fori_loop(0, rows, row, 0)
        forward = forth_ref[...]
        if not with_back:
            return forward, None
        named = lax.broadcasted_iota(jnp.int32, (blocks, rows * tiles_row), 0) == cols_row_ref[...]
        spread = jnp.dot(named.astype(jnp.float32), back_ref[...], precision=EXACT, preferred_element_type=jnp.float32)
        return forward, spread

    def total_of(values):
        return jnp.sum(values, axis=(0, 1), keepdims=True)

    def thirds(values):
        high = values.astype(jnp.bfloat16)
        rest = values - high.astype(jnp.float32)
        middle = rest.astype(jnp.bfloat16)
        return high, middle, (rest - middle.astype(jnp.float32)).astype(jnp.bfloat16)

    lanes = lax.broadcasted_iota(jnp.int32, (width_y, depth_z), 1)
    lines = lax.broadcasted_iota(jnp.int32, (width_y, depth_z), 0)
    next_mat, prev_mat = lax.rem(me_mat + 1, n_mat), lax.rem(me_mat + n_mat - 1, n_mat)
    next_frac, prev_frac = lax.rem(me + 1, n_frac), lax.rem(me + n_frac - 1, n_frac)
    halos = {}

    def send_halo(sweep, last, first):
        sems = [(halo_send.at[sweep, d], halo_recv.at[sweep, d]) for d in range(4)]
        halos[sweep] = [
            send(last, grid_ref.at[sweep, 0], *sems[0], {"mat": next_mat}),
            send(first, grid_ref.at[sweep, width_x + 1], *sems[1], {"mat": prev_mat}),
            send(edge_ref.at[sweep, 0], side_ref.at[sweep, 0], *sems[2], {"frac": next_frac}),
            send(edge_ref.at[sweep, 1], side_ref.at[sweep, 1], *sems[3], {"frac": prev_frac}),
        ]

    def wait_halo(sweep):
        for copy in halos[sweep]:
            copy.wait_recv()
        grid_ref[sweep, 0] = jnp.where(me_mat == 0, 0.0, grid_ref[sweep, 0])
        grid_ref[sweep, width_x + 1] = jnp.where(me_mat == n_mat - 1, 0.0, grid_ref[sweep, width_x + 1])
        side_ref[sweep, 0] = jnp.where(me == 0, 0.0, side_ref[sweep, 0])
        side_ref[sweep, 1] = jnp.where(me == n_frac - 1, 0.0, side_ref[sweep, 1])

    def tz_inner(x):
        return jnp.where(lanes == depth_z - 1, 0.0, face_ref[2, x])

    def set_inverse():
        for copy in coef_copies:
            copy.wait_recv()
        tx_ref[0] = jnp.where(me_mat == 0, 0.0, tx_ref[0])
        ty_side_ref[...] = jnp.where(me == 0, 0.0, ty_side_ref[...])

        def plane(x, carry):
            tx_here, ty_here = face_ref[0, x], face_ref[1, x]
            tx_ref[x + 1] = tx_here
            ty_low = jnp.where(lines == 0, ty_side_ref[pl.ds(x, 1), :], pltpu.roll(ty_here, 1, 0))
            tz_low = pltpu.roll(tz_inner(x), 1, 1)
            inv_ref[x] = relax_weight / (cell_ref[x] + tx_here + tx_ref[x] + ty_here + ty_low + face_ref[2, x] + tz_low)
            return carry

        lax.fori_loop(0, width_x, plane, 0)

    def sweep_part(sweep, low, high):
        def plane(x, carry):
            here = grid_ref[sweep, x + 1]
            ty_here, tz_here = face_ref[1, x], tz_inner(x)
            up = jnp.where(lines == width_y - 1, side_ref[sweep, 1, pl.ds(x, 1), :], pltpu.roll(here, width_y - 1, 0))
            down = jnp.where(
                lines == 0,
                ty_side_ref[pl.ds(x, 1), :] * side_ref[sweep, 0, pl.ds(x, 1), :],
                pltpu.roll(ty_here * here, 1, 0),
            )
            total = base_ref[x] + tx_ref[x + 1] * grid_ref[sweep, x + 2] + tx_ref[x] * grid_ref[sweep, x]
            total = total + ty_here * up + down
            total = total + tz_here * pltpu.roll(here, depth_z - 1, 1) + pltpu.roll(tz_here * here, 1, 1)
            value = (1.0 - relax_weight) * here + inv_ref[x] * total
            if sweep + 1 < sweeps:
                grid_ref[sweep + 1, x + 1] = value
                edge_ref[sweep + 1, 0, pl.ds(x, 1), :] = value[width_y - 1 :]
                edge_ref[sweep + 1, 1, pl.ds(x, 1), :] = value[:1]
            else:
                out_ref[x] = value
            return carry

        lax.fori_loop(low, high, plane, 0)

    quarter = width_x // 4

    def set_sources(low, parts):
        hot = row_hot_ref[low * width_y : (low + quarter) * width_y, :]
        total = sum(
            lax.dot_general(hot, part, (((1,), (1,)), ((), ())), preferred_element_type=jnp.float32) for part in parts
        )
        base_ref[low : low + quarter] = msource_ref[low : low + quarter] + total.reshape(quarter, width_y, depth_z)

    def add_sweep(sweep):
        pieces.append(lambda: wait_halo(sweep))
        for q in range(4):
            pieces.append(functools.partial(sweep_part, sweep, q * quarter, (q + 1) * quarter))
        if sweep + 1 < sweeps:
            pieces.append(
                lambda: send_halo(sweep + 1, grid_ref.at[sweep + 1, width_x], grid_ref.at[sweep + 1, 1])
            )

    def traces(sweep):
        found = []
        cut = slots // 4
        parts = thirds(grid_ref[sweep, 1 : width_x + 1].reshape(width_x * width_y, depth_z))
        for q in range(4):
            hot = row_hot_ref[:, q * cut : (q + 1) * cut]
            picked = sum(
                lax.dot_general(part, hot, (((0,), (0,)), ((), ())), preferred_element_type=jnp.float32)
                for part in parts
            )
            mask = lane_hot_ref[:, q * cut : (q + 1) * cut].astype(jnp.float32)
            found.append(jnp.sum(picked * mask, axis=0, keepdims=True))
        return jnp.concatenate(found, axis=1)

    begin = begin_ref[...]
    first_copies = gather(0, begin)
    grid_ref[0, 1 : width_x + 1] = press_ref[...]
    edge_ref[0, 0] = press_ref[:, width_y - 1, :]
    edge_ref[0, 1] = press_ref[:, 0, :]
    ty_edge_ref[...] = face_ref[1, :, width_y - 1, :]
    coef_copies = [
        send(face_ref.at[0, width_x - 1], tx_ref.at[0], halo_send.at[sweeps, 0], halo_recv.at[sweeps, 0], {"mat": next_mat}),
        send(ty_edge_ref, ty_side_ref, halo_send.at[sweeps, 2], halo_recv.at[sweeps, 2], {"frac": next_frac}),
    ]
    send_halo(0, press_ref.at[width_x - 1], press_ref.at[0])
    place = place_ref[...]
    block_of = place // size_b
    lane_of = place - block_of * size_b
    by_block = (lax.broadcasted_iota(jnp.int32, (blocks, slots), 0) == block_of).astype(jnp.float32)
    by_lane = (lax.broadcasted_iota(jnp.int32, (size_b, slots), 0) == lane_of).astype(jnp.float32)
    cell = where_ref[...]
    cell_row = cell // depth_z
    cell_lane = cell - cell_row * depth_z

    row_hot_ref[...] = (lax.broadcasted_iota(jnp.int32, row_hot_ref.shape, 0) == cell_row).astype(jnp.float32).astype(jnp.bfloat16)
    lane_hot_ref[...] = (lax.broadcasted_iota(jnp.int32, lane_hot_ref.shape, 0) == cell_lane).astype(jnp.float32).astype(jnp.bfloat16)

    diag = diag_ref[...]
    for outer_no in range(OUTER):
        first = outer_no == 0
        stage = outer_no * phases
        trace = traces(outer_no * SWEEPS)
        if first:
            for copy in first_copies:
                copy.wait_recv()
            fracture = gather_ref[0]
        picked = lax.dot_general(fracture, by_block, (((0,), (0,)), ((), ())), precision=EXACT, preferred_element_type=jnp.float32)
        flux = kappa_ref[...] * (trace - jnp.sum(picked * by_lane, axis=0, keepdims=True))
        landed = lax.dot_general(by_block * flux, by_lane, (((1,), (1,)), ((), ())), precision=EXACT, preferred_element_type=jnp.float32)
        if first:
            forward, spread = products(0, True)
        for k in range(n_frac):
            if first:
                outgo_ref[stage, k, 0:rows, :] = spread[k * rows : (k + 1) * rows]
            outgo_ref[stage, k, rows : 2 * rows, :] = landed[k * rows : (k + 1) * rows]
        parts = [lane_hot_ref[...] * part for part in thirds(flux)]
        if first:
            pieces.append(set_inverse)
        for q in range(4):
            pieces.append(functools.partial(set_sources, q * quarter, parts))
        for s in range(SWEEPS):
            add_sweep(outer_no * SWEEPS + s)
        both = exchange(stage, 0 if first else rows, 2 * rows, 2)
        if first:
            image = diag * begin + 0.5 * (forward + both[0:rows])
        mat_ref[outer_no, me_mat] = both[rows:] if first else both
        slot = mat_ref.at[outer_no, me_mat]
        copies = [
            send(slot, slot, mat_send.at[outer_no, k - 1], mat_recv.at[outer_no, k - 1], {"mat": lax.rem(me_mat + k, n_mat)})
            for k in range(1, n_mat)
        ]
        fill(2)
        for copy in copies:
            copy.wait_recv()
        load = mat_ref[outer_no, 0]
        for k in range(1, n_mat):
            load = load + mat_ref[outer_no, k]
        if first:
            residual = fsource_ref[...] + load - image
        else:
            residual = residual + (load - loaded)
        loaded = load

        for step in range(CG_ITERS):
            phase = stage + step + 1
            needed = first or step + 1 < CG_ITERS
            copies = gather(phase, residual)
            fill(2)
            for copy in copies:
                copy.wait_recv()
            whole = gather_ref[phase]
            forward, spread = products(phase, needed)
            inner = residual * (diag * residual + forward)
            for k in range(n_frac):
                if needed:
                    outgo_ref[phase, k, 0:rows, :] = spread[k * rows : (k + 1) * rows]
                outgo_ref[phase, k, rows : 2 * rows, :] = inner
            both = exchange(phase, 0 if needed else rows, 2 * rows, 3)
            if needed:
                image = diag * residual + 0.5 * (forward + both[0:rows])
                product = total_of(both[rows : 2 * rows])
            else:
                product = total_of(both)
            norm_next = total_of(whole * whole)
            if step == 0:
                alpha = norm_next / product
                direction = whole
                along = image
            else:
                ratio = norm_next / norm_now
                alpha = norm_next / (product - ratio * norm_next / alpha)
                direction = whole + ratio * direction
                if needed:
                    along = image + ratio * along
            norm_now = norm_next
            fracture = fracture + alpha * direction
            if needed:
                residual = residual - alpha * along
        fill(len(pieces))
    flux_ref[...] = flux
    gather_ref[phases] = fracture
    own_ref[...] = gather_ref[phases, mine, :]
    for copy in sent:
        copy.wait_send()


def coupled(pressure, face, cell_coef, matrix_source, cells, kappa, place, tiles, tile_cols, diag, begin, fsource):
    n_frac, n_mat = lax.axis_size("frac"), lax.axis_size("mat")
    rows, tiles_row, size_b = tiles.shape[0], tiles.shape[1], tiles.shape[3]
    blocks = rows * n_frac
    x, y, z = pressure.shape
    slots = cells.shape[1]
    f32 = jnp.float32
    vmem = pl.BlockSpec(memory_space=pltpu.VMEM)
    smem = pl.BlockSpec(memory_space=pltpu.SMEM)
    phases = OUTER * (CG_ITERS + 1)
    sweeps = OUTER * SWEEPS
    dma = pltpu.SemaphoreType.DMA
    return pl.pallas_call(
        functools.partial(coupled_kernel, n_frac, n_mat),
        out_shape=(
            jax.ShapeDtypeStruct((x, y, z), f32),
            jax.ShapeDtypeStruct((rows, size_b), f32),
            jax.ShapeDtypeStruct((1, slots), f32),
        ),
        in_specs=[vmem] * 8 + [smem] + [vmem] * 4,
        out_specs=(vmem,) * 3,
        scratch_shapes=[
            pltpu.VMEM((phases, blocks, size_b), f32),
            pltpu.VMEM((phases, n_frac, 2 * rows, size_b), f32),
            pltpu.VMEM((phases, n_frac, 2 * rows, size_b), f32),
            pltpu.VMEM((OUTER, n_mat, rows, size_b), f32),
            pltpu.VMEM((rows * tiles_row, size_b), f32),
            pltpu.VMEM((rows, size_b), f32),
            pltpu.VMEM((sweeps, x + 2, y, z), f32),
            pltpu.VMEM((x + 1, y, z), f32),
            pltpu.VMEM((x, y, z), f32),
            pltpu.VMEM((x, y, z), f32),
            pltpu.VMEM((x * y, slots), jnp.bfloat16),
            pltpu.VMEM((z, slots), jnp.bfloat16),
            pltpu.VMEM((sweeps, 2, x, z), f32),
            pltpu.VMEM((sweeps, 2, x, z), f32),
            pltpu.VMEM((x, z), f32),
            pltpu.VMEM((x, z), f32),
            dma((phases, n_frac - 1)),
            dma((phases, n_frac - 1)),
            dma((phases, n_frac - 1)),
            dma((phases, n_frac - 1)),
            dma((OUTER, n_mat - 1)),
            dma((OUTER, n_mat - 1)),
            dma((sweeps + 1, 4)),
            dma((sweeps + 1, 4)),
        ],
        compiler_params=pltpu.CompilerParams(
            collective_id=0, has_side_effects=True, vmem_limit_bytes=60 * 1024 * 1024
        ),
        name="coupled",
    )(pressure, face, cell_coef, matrix_source, cells, kappa, place, tiles, tile_cols, tile_cols.reshape(1, -1), diag, begin, fsource)


def body(
    pressure_start,
    face_trans,
    cell_coef,
    matrix_source,
    mortar_owner,
    mortar_cell,
    mortar_frac,
    mortar_kappa,
    tiles,
    tile_cols,
    frac_diag,
    frac_source,
    fracture_start,
):
    mat_count = lax.axis_size("mat")
    frac_count = lax.axis_size("frac")
    devices = mat_count * frac_count
    size_b = tiles.shape[2]
    owner = mortar_owner[:, 0]
    mortar_count = owner.shape[0]
    capacity = max(2, 2 * mortar_count // devices)
    hits = (owner[:, None] == jnp.arange(devices, dtype=jnp.int32)[None, :]).astype(jnp.int32)
    ranks = jnp.cumsum(hits, axis=0)
    slot = jnp.sum(ranks * hits, axis=1) - 1
    place = owner * capacity + slot
    slots = devices * capacity
    at_slot = (place[:, None] == jnp.arange(slots, dtype=jnp.int32)[None, :]).astype(jnp.float32)
    payload = jnp.stack([mortar_cell.astype(jnp.float32), mortar_frac.astype(jnp.float32), mortar_kappa])
    outgoing = jnp.dot(payload, at_slot, precision=EXACT).reshape(3, devices, capacity)
    incoming = lax.all_to_all(outgoing, ("mat", "frac"), split_axis=1, concat_axis=1, tiled=True)
    cell_slots = jnp.round(incoming[0]).astype(jnp.int32).reshape(1, -1)
    frac_slots = jnp.round(incoming[1]).astype(jnp.int32).reshape(1, -1)
    kappa_slots = incoming[2].reshape(1, -1)
    blocked = (-1, size_b)
    pressure, fracture, flux = coupled(
        pressure_start,
        face_trans,
        cell_coef,
        matrix_source,
        cell_slots,
        kappa_slots,
        frac_slots,
        tiles,
        tile_cols,
        frac_diag.reshape(blocked),
        fracture_start.reshape(blocked),
        frac_source.reshape(blocked),
    )
    returned = lax.all_to_all(
        flux.reshape(devices, capacity), ("mat", "frac"), split_axis=0, concat_axis=0, tiled=True
    )
    return (pressure, fracture.reshape(-1), returned.reshape(-1)[place])


def solution(mesh):
    in_specs = (
        P("mat", "frac", None),
        P(None, "mat", "frac", None),
        P("mat", "frac", None),
        P("mat", "frac", None),
        P(("mat", "frac"), None),
        P(("mat", "frac")),
        P(("mat", "frac")),
        P(("mat", "frac")),
        P("frac", None, None, None),
        P("frac", None),
        P("frac"),
        P("frac"),
        P("frac"),
    )
    out_specs = (P("mat", "frac", None), P("frac"), P(("mat", "frac")))
    return jax.shard_map(body, mesh=mesh, in_specs=in_specs, out_specs=out_specs, check_vma=False)
```

profile of v0, /device:TPU:0, one launch (start us, length us, event | category | flops | bytes accessed | tf_op | source)
XLA Modules:
  0.0 133.0 jit_solution(8462458740805564474)
XLA Ops:
  0.6 0.7 fusion.4
  1.3 1.2 reduce-window.6
  2.5 0.2 slice_reduce_fusion
  2.7 0.8 fusion.3
  3.5 0.7 compare_select_fusion
  4.2 0.7 convert_element_type.38
  4.9 0.7 convert_element_type.39
  5.6 1.5 %fusion = f32[3,1024]{1,0:T(4,128)S(1)} fusion(s32[512]{0:T(512)S(1)} %bitcast.38, f32[1,512]{1,0:T(1,128)} %bitcast.39, f32[1,512]{1,0:T(1,128)S(1)} %bitcast.37, f32[1,512]{1,0:T(1,128)S(1)} %bitcast.36), kind=kOutput, calls=%fused_computation.2 | convolution fusion | flops 19401728 | bytes 20480 | tf_op jit(solution)/shard_map/dot_general | solution.py:413
  7.1 0.1 reshape.91
  7.2 0.7 copy.22
  7.9 7.3 %all-to-all-start = ((f32[3,32,32]{2,0,1:T(4,128)}), f32[3,32,32]{2,0,1:T(4,128)S(1)}, u32[]{:S(2)}, u32[]{:S(2)}) async-start(f32[3,32,32]{2,0,1:T(4,128)} %copy.22), calls=%async_computation | async-start | bytes 131072 | tf_op jit(solution)/shard_map/all_to_all | solution.py:414
  15.2 0.8 copy.24.refs_8_
  16.0 0.0 copy-start.1
  16.0 0.6 reshape.92.refs_9_
  16.5 5.9 %all-to-all-done = f32[3,32,32]{2,0,1:T(4,128)S(1)} async-done(((f32[3,32,32]{2,0,1:T(4,128)}), f32[3,32,32]{2,0,1:T(4,128)S(1)}, u32[]{:S(2)}, u32[]{:S(2)}) %all-to-all-start) | async-done | bytes 12320 | tf_op jit(solution)/shard_map/all_to_all | solution.py:414
  22.5 0.1 fusion.6
  22.6 0.7 convert_element_type.42.refs_4_
  23.2 0.7 convert_element_type.44.refs_6_
  23.9 0.1 slice_reduce_fusion.1
  24.0 0.7 reshape_squeeze.3.refs_5_
  24.6 0.0 copy-done.1
  24.6 90.4 %coupled.1 = (f32[16,64,256]{2,1,0:T(8,128)}, f32[8,128]{1,0:T(8,128)}, f32[1,1024]{1,0:T(1,128)}) custom-call(f32[16,64,256]{2,1,0:T(8,128)} %refs_0_.1, f32[3,16,64,256]{3,2,1,0:T(8,128)} %refs_1_.1, f32[16,64,256]{2,1,0:T(8,128)} %refs_2_.1, f32[16,64,256]{2,1,0:T(8,128)} %refs_3_.1, s32[1,1024]{1,0:T(1,128)} %convert_element_type.42.refs_4_, ...), custom_call_target="tpu_custom_call" | custom-call | tf_op jit(solution)/shard_map/coupled/pallas_call | solution.py:342
  115.0 0.0 copy-start
  115.0 0.5 broadcast.57
  115.6 1.3 %reduce.20 = f32[1024]{0:T(1024)S(1)} reduce(f32[1,1024]{1,0:T(1,128)} %get-tuple-element.8, f32[]{:T(128)} %broadcast.57), dimensions={0}, to_apply=%get-tuple-element.8.reduce_sub_computation.3 | reduce | bytes 8196 | tf_op jit(solution)/shard_map/coupled/pallas_call | solution.py:342
  116.9 0.7 all_to_all.10
  117.6 2.5 %all-to-all-start.1 = ((f32[32,1,32]{2,1,0:T(1,128)}), f32[32,1,32]{2,1,0:T(1,128)S(1)}, u32[]{:S(2)}, u32[]{:S(2)}) async-start(f32[32,1,32]{2,1,0:T(1,128)} %bitcast.12), calls=%async_computation.1 | async-start | bytes 32768 | tf_op jit(solution)/shard_map/all_to_all | solution.py:433
  120.1 7.1 %all-to-all-done.1 = f32[32,1,32]{2,1,0:T(1,128)S(1)} async-done(((f32[32,1,32]{2,1,0:T(1,128)}), f32[32,1,32]{2,1,0:T(1,128)S(1)}, u32[]{:S(2)}, u32[]{:S(2)}) %all-to-all-start.1) | async-done | bytes 4128 | tf_op jit(solution)/shard_map/all_to_all | solution.py:433
  127.2 0.7 reduce.21
  127.9 0.1 reshape.97
  128.0 0.0 copy-start.2
  128.0 3.4 %gather_fusion = f32[512]{0:T(512)} fusion(f32[1024]{0:T(1024)S(1)} %reshape.97, s32[1024]{0:T(1024)S(1)} %pad_clamp_fusion), kind=kCustom, calls=%fused_computation | custom fusion | bytes 6144 | tf_op jit(solution)/shard_map/gather | solution.py:436
  131.4 0.0 copy-done
  131.4 1.0 copy.30
  132.4 0.0 copy-done.2
  132.4 0.6 copy.31
  (4 shorter events, 0.1 us)
Async XLA Ops:
  7.9 14.6 %all-to-all-start = ((f32[3,32,32]{2,0,1:T(4,128)}), f32[3,32,32]{2,0,1:T(4,128)S(1)}, u32[]{:S(2)}, u32[]{:S(2)}) async-start(f32[3,32,32]{2,0,1:T(4,128)} %copy.22), calls=%async_computation | async-start | bytes 131072 | tf_op jit(solution)/shard_map/all_to_all | solution.py:414
  16.0 8.7 %copy-start.1 = (s32[8,4]{1,0:T(8,128)}, s32[8,4]{1,0:T(8,128)S(1)}, u32[]{:S(2)}) copy-start(s32[8,4]{1,0:T(8,128)S(1)} %copy.24.refs_8_) | copy-start | bytes 388
  115.0 16.3 %copy-start = (f32[16,64,256]{2,1,0:T(8,128)S(1)}, f32[16,64,256]{2,1,0:T(8,128)}, u32[]{:S(2)}) copy-start(f32[16,64,256]{2,1,0:T(8,128)} %get-tuple-element.16) | copy-start | bytes 3145732
  117.6 9.6 %all-to-all-start.1 = ((f32[32,1,32]{2,1,0:T(1,128)}), f32[32,1,32]{2,1,0:T(1,128)S(1)}, u32[]{:S(2)}, u32[]{:S(2)}) async-start(f32[32,1,32]{2,1,0:T(1,128)} %bitcast.12), calls=%async_computation.1 | async-start | bytes 32768 | tf_op jit(solution)/shard_map/all_to_all | solution.py:433
  128.0 4.4 %copy-start.2 = (f32[8,128]{1,0:T(8,128)S(1)}, f32[8,128]{1,0:T(8,128)}, u32[]{:S(2)}) copy-start(f32[8,128]{1,0:T(8,128)} %get-tuple-element.7) | copy-start | bytes 12292
where the time goes:
time: 133 us
  Pallas kernels  90.4 us (68%)
  waiting for transfers between devices  13 us (10%)
  local copies, waits for them, and re-layouts  10.7 us (8%)
  starting transfers between devices  9.87 us (7%)
  other arithmetic  6.86 us (5%)
  matrix products  1.5 us (1%)
    pallas_call x1, Pallas kernels, coupled(): pl.pallas_call(functools.partial(coupled_kernel, n_frac, n_mat), out_shap...  90.4 us
    all_to_all x1, starting transfers between devices, body(): lax.all_to_all(outgoing, ('mat', 'frac'), split_axis=1, concat_axis=1, ti...  7.33 us
    all_to_all x1, waiting for transfers between devices, body(): lax.all_to_all(flux.reshape(devices, capacity), ('mat', 'frac'), split_ax...  7.06 us
    all_to_all x1, waiting for transfers between devices, body(): lax.all_to_all(outgoing, ('mat', 'frac'), split_axis=1, concat_axis=1, ti...  5.92 us
    gather x1, local copies, waits for them, and re-layouts, body(): return (pressure, fracture.reshape(-1), returned.reshape(-1)[place])  3.41 us
  transfers between devices with their start and end apart: 2, of which 2 were waited for; matrix products, arithmetic and copies ran while one was open for 1% of the time, Pallas kernels for 0%

commit v1 on v0

v1 whole, which is shorter than its diff:
```python
import functools

import jax
import jax.numpy as jnp
from jax import lax
from jax.experimental import pallas as pl
from jax.experimental.pallas import tpu as pltpu
from jax.sharding import PartitionSpec as P

SWEEPS = 2
CG_ITERS = 3
OUTER = 2

MESH = pl.DeviceIdType.MESH
LANES = 128

relax_weight = 0.8


def split_parts(values, count):
    parts = []
    for _ in range(count - 1):
        part = values.astype(jnp.bfloat16)
        parts.append(part)
        values = values - part.astype(jnp.float32)
    parts.append(values.astype(jnp.bfloat16))
    return parts


def as_hot(mask):
    return mask.astype(jnp.float32).astype(jnp.bfloat16)


def dot_nn(a, b):
    return lax.dot_general(a, b, (((1,), (0,)), ((), ())), preferred_element_type=jnp.float32)


def dot_nt(a, b):
    return lax.dot_general(a, b, (((1,), (1,)), ((), ())), preferred_element_type=jnp.float32)


def total_of(values):
    return jnp.sum(values, axis=(0, 1), keepdims=True)


def coupled_kernel(n_frac, n_mat, *refs):
    (press_hbm, face_hbm, cell_hbm, msource_hbm, tiles_hbm, owner_ref, cells_ref, places_ref, kappa_in_ref, cols_ref,
     diag_ref, begin_ref, fsource_ref, out_hbm, own_ref, flux_out_ref, *scratch) = refs
    (grid_ref, tx_ref, ty_ref, tz_ref, inv_ref, cell_ref, msource_ref, base_ref, result_ref, tiles_ref, parts_ref,
     row_hot_ref, lane_hot_ref, side_ref, edge_ref, ty_edge_ref, ty_side_ref, mort_out_ref, mort_in_ref, vec_ref,
     dest_out_ref, dest_in_ref, mv_ref, vector_ref, rs_out_0, rs_in_0, ag_0, rs_out_1, rs_in_1, ag_1, part_out_ref, part_in_ref,
     back_out_ref, back_in_ref, local_sem, out_sem, mort_send, mort_recv, vec_send, vec_recv, mv_send, mv_recv,
     rs_send, rs_recv, ag_send, ag_recv, part_send, part_recv, back_send, back_recv, halo_send, halo_recv) = scratch
    rows, tiles_row, size_b = tiles_ref.shape[0], tiles_ref.shape[1], tiles_ref.shape[3]
    width_x, width_y, depth_z = inv_ref.shape
    grid_rows = width_x * width_y
    mortars = owner_ref.shape[1]
    devices = n_mat * n_frac
    capacity = 2 * mortars // devices
    per = LANES // capacity
    groups = devices // per
    slots = devices * capacity
    blocks = rows * n_frac
    tiles_all = rows * tiles_row
    lines_mv = tiles_all + rows
    share = blocks // devices
    sweeps = OUTER * SWEEPS
    f32, i32 = jnp.float32, jnp.int32
    me = lax.axis_index("frac")
    me_mat = lax.axis_index("mat")
    me_dev = me_mat * n_frac + me
    everyone = [(c, k) for c in range(n_mat) for k in range(n_frac) if c or k]

    barrier = pltpu.get_barrier_semaphore()
    for c, k in everyone:
        pl.semaphore_signal(
            barrier,
            inc=1,
            device_id={"mat": lax.rem(me_mat + c, n_mat), "frac": lax.rem(me + k, n_frac)},
            device_id_type=MESH,
        )

    def load(index, src, dst):
        copy = pltpu.make_async_copy(src, dst, local_sem.at[index])
        copy.start()
        return copy

    press_copy = load(0, press_hbm, grid_ref.at[0, pl.ds(1, width_x)])
    tx_copy = load(1, face_hbm.at[0], tx_ref.at[pl.ds(1, width_x)])
    ty_copy = load(2, face_hbm.at[1], ty_ref)
    tiles_copy = load(3, tiles_hbm, tiles_ref)
    tz_copy = load(4, face_hbm.at[2], tz_ref)
    cell_copy = load(5, cell_hbm, cell_ref)
    msource_copy = load(6, msource_hbm, msource_ref)

    sent = []

    def send(src, dst, send_sem, recv_sem, device):
        copy = pltpu.make_async_remote_copy(
            src_ref=src, dst_ref=dst, send_sem=send_sem, recv_sem=recv_sem, device_id=device, device_id_type=MESH
        )
        copy.start()
        return copy

    def take(ref, sem):
        pltpu.make_async_copy(ref, ref, sem).wait()

    def spread_to_all(source, landing, send_sem, recv_sem):
        for c, k in everyone:
            mat, frac = lax.rem(me_mat + c, n_mat), lax.rem(me + k, n_frac)
            send(source(mat * n_frac + frac), landing.at[me_dev], send_sem, recv_sem, {"mat": mat, "frac": frac})
        sent.append((landing.at[pl.ds(0, devices - 1)], send_sem))

    def spread_to_frac(source, landing, send_sem, recv_sem):
        for k in range(1, n_frac):
            send(source, landing.at[me], send_sem, recv_sem, {"frac": lax.rem(me + k, n_frac)})
        sent.append((landing.at[pl.ds(0, n_frac - 1)], send_sem))

    owner = owner_ref[...]
    named = lax.broadcasted_iota(i32, (devices, mortars), 0) == owner
    named_hot = as_hot(named)
    before = as_hot(lax.broadcasted_iota(i32, (mortars, mortars), 0) <= lax.broadcasted_iota(i32, (mortars, mortars), 1))
    counts = dot_nn(named_hot, before)
    rank = jnp.sum(jnp.where(named, counts, 0.0), axis=0, keepdims=True).astype(i32) - 1
    spot = lax.broadcasted_iota(i32, (LANES, mortars), 0)
    word = lax.rem(spot // capacity + (per - lax.rem(me_dev, per)), per)
    payload = jnp.where(word == 0, cells_ref[...].astype(f32), jnp.where(word == 1, places_ref[...].astype(f32), kappa_in_ref[...]))
    payload = jnp.where((word < 3) & (lax.rem(spot, capacity) == rank), payload, 0.0)
    outgoing = sum(dot_nt(named_hot, part) for part in split_parts(payload, 3))
    mort_out_ref[...] = outgoing.reshape(devices, 1, LANES)

    lane_line = lax.broadcasted_iota(i32, (1, LANES), 1)
    target_row = jnp.where((lane_line >= tiles_all) & (lane_line < lines_mv), me * rows + lane_line - tiles_all, -1)
    for r in range(rows):
        for t in range(tiles_row):
            target_row = jnp.where(lane_line == r * tiles_row + t, cols_ref[t, r], target_row)
    dest_out_ref[...] = target_row.astype(f32)

    pl.semaphore_wait(barrier, devices - 1)
    spread_to_all(lambda target: mort_out_ref.at[target], mort_in_ref, mort_send, mort_recv)
    mort_in_ref[me_dev] = mort_out_ref[me_dev]
    spread_to_frac(begin_ref, vec_ref.at[0], vec_send.at[0], vec_recv.at[0])
    spread_to_frac(dest_out_ref, dest_in_ref, vec_send.at[3], vec_recv.at[3])
    vec_ref[0, me] = begin_ref[...]
    dest_in_ref[me] = dest_out_ref[...]

    lanes = lax.broadcasted_iota(i32, (width_y, depth_z), 1)
    lines = lax.broadcasted_iota(i32, (width_y, depth_z), 0)
    next_mat, prev_mat = lax.rem(me_mat + 1, n_mat), lax.rem(me_mat + n_mat - 1, n_mat)
    next_frac, prev_frac = lax.rem(me + 1, n_frac), lax.rem(me + n_frac - 1, n_frac)
    halos = {}
    slow_sends = []

    def send_halo(sweep):
        sems = [(halo_send.at[sweep, d], halo_recv.at[sweep, d]) for d in range(4)]
        halos[sweep] = [
            send(grid_ref.at[sweep, width_x], grid_ref.at[sweep, 0], *sems[0], {"mat": next_mat}),
            send(grid_ref.at[sweep, 1], grid_ref.at[sweep, width_x + 1], *sems[1], {"mat": prev_mat}),
            send(edge_ref.at[sweep, 0], side_ref.at[sweep, 0], *sems[2], {"frac": next_frac}),
            send(edge_ref.at[sweep, 1], side_ref.at[sweep, 1], *sems[3], {"frac": prev_frac}),
        ]
        slow_sends.extend(halos[sweep])

    def wait_halo(sweep):
        for copy in halos[sweep]:
            copy.wait_recv()
        grid_ref[sweep, 0] = jnp.where(me_mat == 0, 0.0, grid_ref[sweep, 0])
        grid_ref[sweep, width_x + 1] = jnp.where(me_mat == n_mat - 1, 0.0, grid_ref[sweep, width_x + 1])
        side_ref[sweep, 0] = jnp.where(me == 0, 0.0, side_ref[sweep, 0])
        side_ref[sweep, 1] = jnp.where(me == n_frac - 1, 0.0, side_ref[sweep, 1])

    press_copy.wait()
    edge_ref[0, 0] = grid_ref[0, 1 : width_x + 1, width_y - 1, :]
    edge_ref[0, 1] = grid_ref[0, 1 : width_x + 1, 0, :]
    send_halo(0)
    tx_copy.wait()
    ty_copy.wait()
    ty_edge_ref[...] = ty_ref[:, width_y - 1, :]
    coef_copies = [
        send(tx_ref.at[width_x], tx_ref.at[0], halo_send.at[sweeps, 0], halo_recv.at[sweeps, 0], {"mat": next_mat}),
        send(ty_edge_ref, ty_side_ref, halo_send.at[sweeps, 2], halo_recv.at[sweeps, 2], {"frac": next_frac}),
    ]
    slow_sends.extend(coef_copies)
    spread_to_frac(fsource_ref, vec_ref.at[1], vec_send.at[1], vec_recv.at[1])
    spread_to_frac(diag_ref, vec_ref.at[2], vec_send.at[2], vec_recv.at[2])
    vec_ref[1, me] = fsource_ref[...]
    vec_ref[2, me] = diag_ref[...]

    def gathered(index):
        take(vec_ref.at[index, pl.ds(0, n_frac - 1)], vec_recv.at[index])
        return vec_ref[index].reshape(blocks, size_b)

    def set_parts(sweep):
        high, low = split_parts(grid_ref[sweep, 1 : width_x + 1].reshape(grid_rows, depth_z), 2)
        parts_ref[0] = high
        parts_ref[1] = low

    def set_inverse():
        tz_copy.wait()
        cell_copy.wait()
        for copy in coef_copies:
            copy.wait_recv()
        tx_ref[0] = jnp.where(me_mat == 0, 0.0, tx_ref[0])
        ty_side_ref[...] = jnp.where(me == 0, 0.0, ty_side_ref[...])

        def plane(x, carry):
            ty_here, tz_here = ty_ref[x], tz_ref[x]
            tz_in = jnp.where(lanes == depth_z - 1, 0.0, tz_here)
            ty_low = jnp.where(lines == 0, ty_side_ref[pl.ds(x, 1), :], pltpu.roll(ty_here, 1, 0))
            tz_low = pltpu.roll(tz_in, 1, 1)
            inv_ref[x] = relax_weight / (cell_ref[x] + tx_ref[x + 1] + tx_ref[x] + ty_here + ty_low + tz_here + tz_low)
            tz_ref[x] = tz_in
            return carry

        lax.fori_loop(0, width_x, plane, 0)

    def sweep_part(sweep, low, high):
        def plane(x, carry):
            here = grid_ref[sweep, x + 1]
            ty_here, tz_here = ty_ref[x], tz_ref[x]
            up = jnp.where(lines == width_y - 1, side_ref[sweep, 1, pl.ds(x, 1), :], pltpu.roll(here, width_y - 1, 0))
            down = jnp.where(
                lines == 0,
                ty_side_ref[pl.ds(x, 1), :] * side_ref[sweep, 0, pl.ds(x, 1), :],
                pltpu.roll(ty_here * here, 1, 0),
            )
            total = base_ref[x] + tx_ref[x + 1] * grid_ref[sweep, x + 2] + tx_ref[x] * grid_ref[sweep, x]
            total = total + ty_here * up + down
            total = total + tz_here * pltpu.roll(here, depth_z - 1, 1) + pltpu.roll(tz_here * here, 1, 1)
            value = (1.0 - relax_weight) * here + inv_ref[x] * total
            if sweep + 1 < sweeps:
                grid_ref[sweep + 1, x + 1] = value
                edge_ref[sweep + 1, 0, pl.ds(x, 1), :] = value[width_y - 1 :]
                edge_ref[sweep + 1, 1, pl.ds(x, 1), :] = value[:1]
            else:
                result_ref[x] = value
            return carry

        lax.fori_loop(low, high, plane, 0)

    set_parts(0)
    set_inverse()

    take(mort_in_ref.at[pl.ds(0, devices - 1)], mort_recv)
    arrived = mort_in_ref[...].reshape(devices, LANES)
    window = lax.broadcasted_iota(i32, (devices, LANES), 1) // capacity
    device = lax.broadcasted_iota(i32, (devices, LANES), 0)

    def slot_line(word_no):
        turned = pltpu.roll(arrived, LANES - word_no * capacity, 1) if word_no else arrived
        chosen = jnp.where(lax.rem(device, per) == window, turned, 0.0)
        return jnp.concatenate(
            [jnp.sum(chosen[g * per : (g + 1) * per], axis=0, keepdims=True) for g in range(groups)], axis=1
        )

    cell = slot_line(0).astype(i32)
    place = slot_line(1).astype(i32)
    kappa = slot_line(2)
    cell_row = cell // depth_z
    cell_lane = cell - cell_row * depth_z
    block_of = place // size_b
    lane_of = place - block_of * size_b
    lane_hot_ref[...] = as_hot(lax.broadcasted_iota(i32, (depth_z, slots), 0) == cell_lane)
    by_lane = as_hot(lax.broadcasted_iota(i32, (size_b, slots), 0) == lane_of)
    by_block = lax.broadcasted_iota(i32, (blocks, slots), 0) == block_of

    quarter = slots // 4
    grid_line = lax.broadcasted_iota(i32, (grid_rows, quarter), 0)

    def traces():
        found = []
        for q in range(4):
            hot = lane_hot_ref[:, q * quarter : (q + 1) * quarter]
            picked = dot_nn(parts_ref[0], hot) + dot_nn(parts_ref[1], hot)
            found.append(
                jnp.sum(jnp.where(grid_line == cell_row[:, q * quarter : (q + 1) * quarter], picked, 0.0), axis=0, keepdims=True)
            )
        return jnp.concatenate(found, axis=1)

    def at_slots(values):
        picked = sum(dot_nn(part, by_lane) for part in split_parts(values, 3))
        return jnp.sum(jnp.where(by_block, picked, 0.0), axis=0, keepdims=True)

    def landed(values):
        return sum(dot_nt(as_part, by_lane) for as_part in split_parts(jnp.where(by_block, values, 0.0), 3))

    shares = [(rs_out_0, rs_in_0, ag_0), (rs_out_1, rs_in_1, ag_1)]

    def scatter_share(stage, arrays):
        out, landing, _ = shares[stage]
        for n, array in enumerate(arrays):
            out[:, n] = array.reshape(devices, share, size_b)
        spread_to_all(lambda target: out.at[target], landing, rs_send.at[stage], rs_recv.at[stage])
        landing[me_dev] = out[me_dev]

    def gather_share(stage):
        _, landing, whole = shares[stage]
        take(landing.at[pl.ds(0, devices - 1)], rs_recv.at[stage])
        mine = landing[0]
        for d in range(1, devices):
            mine = mine + landing[d]
        whole[me_dev] = mine
        spread_to_all(lambda target: whole.at[me_dev], whole, ag_send.at[stage], ag_recv.at[stage])

    def whole_shares(stage):
        _, _, whole = shares[stage]
        take(whole.at[pl.ds(0, devices - 1)], ag_recv.at[stage])
        return [whole[:, n].reshape(blocks, size_b) for n in range(whole.shape[1])]

    def products(phase, with_back):
        def row(r, carry):
            across = vector_ref[phase, pl.ds(me * rows + r, 1), :]
            down = jnp.broadcast_to(across, (size_b, size_b)).T
            total = jnp.zeros((size_b, size_b), f32)
            for t in range(tiles_row):
                tile = tiles_ref[r, t]
                total = total + tile * vector_ref[phase, pl.ds(cols_ref[t, r], 1), :]
                if with_back:
                    mv_ref[phase, me, pl.ds(r * tiles_row + t, 1), :] = jnp.sum(tile * down, axis=0, keepdims=True)
            mv_ref[phase, me, pl.ds(tiles_all + r, 1), :] = jnp.sum(total.T, axis=0, keepdims=True)
            return carry

        lax.fori_loop(0, rows, row, 0)

    def start_matvec(phase, vector):
        vector_ref[phase] = vector
        products(phase, True)
        spread_to_frac(mv_ref.at[phase, me], mv_ref.at[phase], mv_send.at[phase], mv_recv.at[phase])

    def finish_matvec(phase, vector):
        take(mv_ref.at[phase, pl.ds(0, n_frac - 1)], mv_recv.at[phase])
        forward = mv_ref[phase, :, tiles_all:].reshape(blocks, size_b)
        product = total_of(vector * (diag * vector + forward))
        arrived = mv_ref[phase].reshape(n_frac * lines_mv, size_b)
        both = sum(dot_nn(targets, part) for part in split_parts(arrived, 3))
        return product, diag * vector + 0.5 * both

    def set_row_hot():
        line = lax.broadcasted_iota(i32, (grid_rows, quarter), 0)
        for q in range(4):
            cut = slice(q * quarter, (q + 1) * quarter)
            row_hot_ref[:, cut] = as_hot(line == cell_row[:, cut])

    part_x = width_x // 4

    def set_sources(flux):
        wide = lane_hot_ref[...]
        weights = [wide * part for part in split_parts(flux, 2)]
        for q in range(4):
            low = q * part_x
            hot = row_hot_ref[low * width_y : (low + part_x) * width_y, :]
            total = sum(dot_nt(hot, weight) for weight in weights)
            base_ref[low : low + part_x] = msource_ref[low : low + part_x] + total.reshape(part_x, width_y, depth_z)

    begin = gathered(0)
    trace = traces()
    flux = kappa * (trace - at_slots(begin))
    scatter_share(0, [landed(flux)])

    tiles_copy.wait()
    start_matvec(0, begin)
    set_row_hot()
    msource_copy.wait()
    set_sources(flux)
    take(dest_in_ref.at[pl.ds(0, n_frac - 1)], vec_recv.at[3])
    block_line = lax.broadcasted_iota(i32, (blocks, LANES), 0)
    targets = jnp.concatenate(
        [as_hot(block_line == dest_in_ref[d].astype(i32))[:, :lines_mv] for d in range(n_frac)], axis=1
    )
    fsource = gathered(1)
    diag = gathered(2)
    gather_share(0)

    wait_halo(0)
    sweep_part(0, 0, width_x)
    send_halo(1)
    _, image = finish_matvec(0, begin)
    (loaded,) = whole_shares(0)
    residual = fsource + loaded - image
    fracture = begin

    def fill(number):
        if number == 0:
            wait_halo(1)
            sweep_part(1, 0, width_x)
            send_halo(2)
            set_parts(2)
            state["trace"] = traces()
            scatter_share(1, [landed(kappa * state["trace"]), landed(kappa)])
        elif number == 2:
            gather_share(1)
        elif number == 3:
            flux = kappa * (state["trace"] - at_slots(state["fracture"]))
            for g in range(groups):
                back_out_ref[g] = flux[:, g * LANES : (g + 1) * LANES]
            spread_to_all(lambda target: back_out_ref.at[target // per], back_in_ref, back_send, back_recv)
            back_in_ref[me_dev] = back_out_ref[me_dev // per]
            set_sources(flux)
            wait_halo(2)
            sweep_part(2, 0, width_x)
            send_halo(3)
        elif number == 4:
            wait_halo(3)
            for q in range(4):
                part = pl.ds(q * part_x, part_x)
                sweep_part(3, q * part_x, (q + 1) * part_x)
                copy = pltpu.make_async_copy(result_ref.at[part], out_hbm.at[part], out_sem.at[q])
                copy.start()
                results.append(copy)
        elif number == 5:
            take(back_in_ref.at[pl.ds(0, devices - 1)], back_recv)
            came = back_in_ref[...].reshape(devices, LANES)
            lines_back = sum(
                lax.dot_general(part, named_hot, (((0,), (0,)), ((), ())), preferred_element_type=f32)
                for part in split_parts(came, 3)
            )
            want = rank + capacity * lax.rem(me_dev, per)
            flux_out_ref[...] = jnp.sum(jnp.where(spot == want, lines_back, 0.0), axis=0, keepdims=True)

    state = {}
    results = []
    last = OUTER * CG_ITERS - 1
    for number in range(OUTER * CG_ITERS):
        step = number % CG_ITERS
        phase = number + 1
        if number == CG_ITERS:
            traced, weight = whole_shares(1)
            residual = residual + ((traced - weight * fracture) - loaded)
            state["fracture"] = fracture
        if number < last:
            start_matvec(phase, residual)
        else:
            vector_ref[phase] = residual
            products(phase, False)
            mine = pl.ds(pl.multiple_of(me * rows, rows), rows)
            part_out_ref[...] = jnp.sum(
                vector_ref[phase, mine, :] * mv_ref[phase, me, tiles_all:, :], axis=0, keepdims=True
            )
            spread_to_frac(part_out_ref, part_in_ref, part_send, part_recv)
            part_in_ref[me] = part_out_ref[...]
        norm_next = total_of(residual * residual)
        fill(number)
        if number < last:
            product, image = finish_matvec(phase, residual)
        else:
            take(part_in_ref.at[pl.ds(0, n_frac - 1)], part_recv)
            product = total_of(diag * residual * residual)
            lines_all = part_in_ref[0]
            for d in range(1, n_frac):
                lines_all = lines_all + part_in_ref[d]
            product = product + total_of(lines_all)
        if step == 0:
            alpha = norm_next / product
            direction = residual
            along = image
        else:
            ratio = norm_next / norm_now
            alpha = norm_next / (product - ratio * norm_next / alpha)
            direction = residual + ratio * direction
            if number < last:
                along = image + ratio * along
        norm_now = norm_next
        fracture = fracture + alpha * direction
        if number < last:
            residual = residual - alpha * along

    vector_ref[0] = fracture
    own_ref[...] = vector_ref[0, pl.ds(pl.multiple_of(me * rows, rows), rows), :]
    for ref, sem in sent:
        take(ref, sem)
    for copy in slow_sends:
        copy.wait_send()
    for copy in results:
        copy.wait()


def coupled(pressure, face, cell_coef, matrix_source, tiles, owner, cells, places, kappa, tile_cols, diag, begin, fsource):
    n_frac, n_mat = lax.axis_size("frac"), lax.axis_size("mat")
    devices = n_frac * n_mat
    rows, tiles_row, size_b = tiles.shape[0], tiles.shape[1], tiles.shape[3]
    blocks = rows * n_frac
    x, y, z = pressure.shape
    mortars = owner.shape[1]
    capacity = 2 * mortars // devices
    slots = devices * capacity
    groups = slots // LANES
    share = blocks // devices
    lines_mv = rows * tiles_row + rows
    f32, bf16 = jnp.float32, jnp.bfloat16
    vmem = pl.BlockSpec(memory_space=pltpu.VMEM)
    smem = pl.BlockSpec(memory_space=pltpu.SMEM)
    hbm = pl.BlockSpec(memory_space=pl.ANY)
    phases = OUTER * CG_ITERS + 1
    sweeps = OUTER * SWEEPS
    dma = pltpu.SemaphoreType.DMA
    return pl.pallas_call(
        functools.partial(coupled_kernel, n_frac, n_mat),
        out_shape=(
            jax.ShapeDtypeStruct((x, y, z), f32),
            jax.ShapeDtypeStruct((rows, size_b), f32),
            jax.ShapeDtypeStruct((1, mortars), f32),
        ),
        in_specs=[hbm] * 5 + [vmem] * 4 + [smem] + [vmem] * 3,
        out_specs=(hbm, vmem, vmem),
        scratch_shapes=[
            pltpu.VMEM((sweeps, x + 2, y, z), f32),
            pltpu.VMEM((x + 1, y, z), f32),
            pltpu.VMEM((x, y, z), f32),
            pltpu.VMEM((x, y, z), f32),
            pltpu.VMEM((x, y, z), f32),
            pltpu.VMEM((x, y, z), f32),
            pltpu.VMEM((x, y, z), f32),
            pltpu.VMEM((x, y, z), f32),
            pltpu.VMEM((x, y, z), f32),
            pltpu.VMEM((rows, tiles_row, size_b, size_b), f32),
            pltpu.VMEM((2, x * y, z), bf16),
            pltpu.VMEM((x * y, slots), bf16),
            pltpu.VMEM((z, slots), bf16),
            pltpu.VMEM((sweeps, 2, x, z), f32),
            pltpu.VMEM((sweeps, 2, x, z), f32),
            pltpu.VMEM((x, z), f32),
            pltpu.VMEM((x, z), f32),
            pltpu.VMEM((devices, 1, LANES), f32),
            pltpu.VMEM((devices, 1, LANES), f32),
            pltpu.VMEM((3, n_frac, rows, size_b), f32),
            pltpu.VMEM((1, LANES), f32),
            pltpu.VMEM((n_frac, 1, LANES), f32),
            pltpu.VMEM((phases, n_frac, lines_mv, size_b), f32),
            pltpu.VMEM((phases, blocks, size_b), f32),
            pltpu.VMEM((devices, 1, share, size_b), f32),
            pltpu.VMEM((devices, 1, share, size_b), f32),
            pltpu.VMEM((devices, 1, share, size_b), f32),
            pltpu.VMEM((devices, 2, share, size_b), f32),
            pltpu.VMEM((devices, 2, share, size_b), f32),
            pltpu.VMEM((devices, 2, share, size_b), f32),
            pltpu.VMEM((1, size_b), f32),
            pltpu.VMEM((n_frac, 1, size_b), f32),
            pltpu.VMEM((groups, 1, LANES), f32),
            pltpu.VMEM((devices, 1, LANES), f32),
            dma((7,)),
            dma((4,)),
            dma,
            dma,
            dma((4,)),
            dma((4,)),
            dma((phases,)),
            dma((phases,)),
            dma((2,)),
            dma((2,)),
            dma((2,)),
            dma((2,)),
            dma,
            dma,
            dma,
            dma,
            dma((sweeps + 1, 4)),
            dma((sweeps + 1, 4)),
        ],
        compiler_params=pltpu.CompilerParams(
            collective_id=0, has_side_effects=True, vmem_limit_bytes=60 * 1024 * 1024
        ),
        name="coupled",
    )(pressure, face, cell_coef, matrix_source, tiles, owner, cells, places, kappa, tile_cols, diag, begin, fsource)


def body(
    pressure_start,
    face_trans,
    cell_coef,
    matrix_source,
    mortar_owner,
    mortar_cell,
    mortar_frac,
    mortar_kappa,
    tiles,
    tile_cols,
    frac_diag,
    frac_source,
    fracture_start,
):
    size_b = tiles.shape[2]
    line = (1, -1)
    blocked = (-1, size_b)
    pressure, fracture, flux = coupled(
        pressure_start,
        face_trans,
        cell_coef,
        matrix_source,
        tiles,
        mortar_owner.reshape(line),
        mortar_cell.reshape(line),
        mortar_frac.reshape(line),
        mortar_kappa.reshape(line),
        tile_cols.T,
        frac_diag.reshape(blocked),
        fracture_start.reshape(blocked),
        frac_source.reshape(blocked),
    )
    return (pressure, fracture.reshape(-1), flux.reshape(-1))


def solution(mesh):
    in_specs = (
        P("mat", "frac", None),
        P(None, "mat", "frac", None),
        P("mat", "frac", None),
        P("mat", "frac", None),
        P(("mat", "frac"), None),
        P(("mat", "frac")),
        P(("mat", "frac")),
        P(("mat", "frac")),
        P("frac", None, None, None),
        P("frac", None),
        P("frac"),
        P("frac"),
        P("frac"),
    )
    out_specs = (P("mat", "frac", None), P("frac"), P(("mat", "frac")))
    return jax.shard_map(body, mesh=mesh, in_specs=in_specs, out_specs=out_specs, check_vma=False)
```

time: 133 us -> 71 us (0.53)
  Pallas kernels: 90.4 us -> 65.4 us
  waiting for transfers between devices: 13 us -> 0 us
  starting transfers between devices: 9.87 us -> 0 us
  other arithmetic: 6.86 us -> 0 us
  local copies, waits for them, and re-layouts: 10.7 us -> 4.8 us
  matrix products: 1.5 us -> 0 us
    pallas_call x1, Pallas kernels: 90.4 us -> 65.4 us  [coupled(): pl.pallas_call(functools.partial(coupled_kernel, n_frac, n_mat), out_shap...]
    all_to_all x2 -> x0, waiting for transfers between devices: 13 us -> none  [the longest x1 7.06 us: body(): lax.all_to_all(flux.reshape(devices, capacity), ('mat', 'frac'), split_ax...]
    all_to_all x2 -> x0, starting transfers between devices: 9.87 us -> none  [the longest x1 7.33 us: body(): lax.all_to_all(outgoing, ('mat', 'frac'), split_axis=1, concat_axis=1, ti...]
    gather x1 -> x0, local copies, waits for them, and re-layouts: 3.41 us -> none  [body(): return (pressure, fracture.reshape(-1), returned.reshape(-1)[place])]
    unnamed x9 -> x3, local copies, waits for them, and re-layouts: 2.33 us -> 4.8 us
    convert_element_type x4 -> x0, other arithmetic: 2.16 us -> none  [the longest x1 0.69 us: body(): (owner[:, None] == jnp.arange(devices, dtype=jnp.int32)[None, :]).astype(...]
    dot_general x1 -> x0, matrix products: 1.5 us -> none  [body(): jnp.dot(payload, at_slot, precision=EXACT).reshape(3, devices, capacity)]
    reshape x4 -> x0, local copies, waits for them, and re-layouts: 1.43 us -> none  [the longest x2 0.76 us: body(): jnp.dot(payload, at_slot, precision=EXACT).reshape(3, devices, capacity)]
  transfers between devices with their start and end apart: 2 -> 0, of which waited for: 2 -> 0; matrix products, arithmetic and copies ran while one was open for 1% -> 0% of each run, Pallas kernels for 0% -> 0%
where the time goes in v1:
time: 71 us; the launch traced here: 70.8 us
  Pallas kernels  65.4 us (92%)
  local copies, waits for them, and re-layouts  4.8 us (7%)
    pallas_call x1, Pallas kernels, coupled(): pl.pallas_call(functools.partial(coupled_kernel, n_frac, n_mat), out_shap...  65.4 us
    unnamed x3, local copies, waits for them, and re-layouts  4.8 us

profile of v1, /device:TPU:0, one launch (start us, length us, event | category | flops | bytes accessed | tf_op | source)
XLA Modules:
  0.0 70.8 jit_solution(1151873981273868335)
XLA Ops:
  0.6 65.4 %coupled.1 = (f32[16,64,256]{2,1,0:T(8,128)}, f32[8,128]{1,0:T(8,128)}, f32[1,512]{1,0:T(1,128)}) custom-call(f32[16,64,256]{2,1,0:T(8,128)} %refs_0_.1, f32[3,16,64,256]{3,2,1,0:T(8,128)} %refs_1_.1, f32[16,64,256]{2,1,0:T(8,128)} %refs_2_.1, f32[16,64,256]{2,1,0:T(8,128)} %refs_3_.1, f32[8,4,128,128]{3,2,1,0:T(8,128)} %refs_4_.1, s32[1,512]{1,0:T(1,128)} %bitcast.14, ...), custom_call_target="tpu_custom_call" | custom-call | tf_op jit(solution)/shard_map/coupled/pallas_call | solution.py:496
  66.0 2.3 %copy.19 = f32[16,64,256]{2,1,0:T(8,128)} copy(f32[16,64,256]{2,1,0:T(8,128)} %get-tuple-element.12) | data formatting | bytes 2097152
  68.3 1.3 %copy.20 = f32[1024]{0:T(1024)} copy(f32[1024]{0:T(1024)} %bitcast.13) | data formatting | bytes 8192
  69.6 1.2 %copy.21 = f32[512]{0:T(512)} copy(f32[512]{0:T(512)} %bitcast.19) | data formatting | bytes 4096

commit v2 on v1

--- a/solution.py
+++ b/solution.py
@@ -45,11 +45,11 @@
 
 def coupled_kernel(n_frac, n_mat, *refs):
     (press_hbm, face_hbm, cell_hbm, msource_hbm, tiles_hbm, owner_ref, cells_ref, places_ref, kappa_in_ref, cols_ref,
-     diag_ref, begin_ref, fsource_ref, out_hbm, own_ref, flux_out_ref, *scratch) = refs
-    (grid_ref, tx_ref, ty_ref, tz_ref, inv_ref, cell_ref, msource_ref, base_ref, result_ref, tiles_ref, parts_ref,
+     diag_ref, begin_ref, fsource_ref, out_ref, own_ref, flux_out_ref, *scratch) = refs
+    (grid_ref, tx_ref, ty_ref, tz_ref, inv_ref, cell_ref, msource_ref, base_ref, tiles_ref, parts_ref,
      row_hot_ref, lane_hot_ref, side_ref, edge_ref, ty_edge_ref, ty_side_ref, mort_out_ref, mort_in_ref, vec_ref,
      dest_out_ref, dest_in_ref, mv_ref, vector_ref, rs_out_0, rs_in_0, ag_0, rs_out_1, rs_in_1, ag_1, part_out_ref, part_in_ref,
-     back_out_ref, back_in_ref, local_sem, out_sem, mort_send, mort_recv, vec_send, vec_recv, mv_send, mv_recv,
+     back_out_ref, back_in_ref, local_sem, mort_send, mort_recv, vec_send, vec_recv, mv_send, mv_recv,
      rs_send, rs_recv, ag_send, ag_recv, part_send, part_recv, back_send, back_recv, halo_send, halo_recv) = scratch
     rows, tiles_row, size_b = tiles_ref.shape[0], tiles_ref.shape[1], tiles_ref.shape[3]
     width_x, width_y, depth_z = inv_ref.shape
@@ -233,13 +233,12 @@
                 edge_ref[sweep + 1, 0, pl.ds(x, 1), :] = value[width_y - 1 :]
                 edge_ref[sweep + 1, 1, pl.ds(x, 1), :] = value[:1]
             else:
-                result_ref[x] = value
+                out_ref[x] = value
             return carry
 
         lax.fori_loop(low, high, plane, 0)
 
     set_parts(0)
-    set_inverse()
 
     take(mort_in_ref.at[pl.ds(0, devices - 1)], mort_recv)
     arrived = mort_in_ref[...].reshape(devices, LANES)
@@ -307,32 +306,47 @@
         take(whole.at[pl.ds(0, devices - 1)], ag_recv.at[stage])
         return [whole[:, n].reshape(blocks, size_b) for n in range(whole.shape[1])]
 
+    half = tiles_all // 2
+
+    def send_lines(phase, low, high):
+        part = pl.ds(low, high - low)
+        for k in range(1, n_frac):
+            send(
+                mv_ref.at[phase, me, part],
+                mv_ref.at[phase, me, part],
+                mv_send.at[phase],
+                mv_recv.at[phase],
+                {"frac": lax.rem(me + k, n_frac)},
+            )
+
     def products(phase, with_back):
-        def row(r, carry):
-            across = vector_ref[phase, pl.ds(me * rows + r, 1), :]
-            down = jnp.broadcast_to(across, (size_b, size_b)).T
-            total = jnp.zeros((size_b, size_b), f32)
+        own = vector_ref[phase, pl.ds(pl.multiple_of(me * rows, rows), rows), :]
+        for r in range(rows):
+            down = jnp.broadcast_to(own[r : r + 1], (size_b, size_b)).T
+            total = None
             for t in range(tiles_row):
                 tile = tiles_ref[r, t]
-                total = total + tile * vector_ref[phase, pl.ds(cols_ref[t, r], 1), :]
+                part = tile * vector_ref[phase, pl.ds(cols_ref[t, r], 1), :]
+                total = part if total is None else total + part
                 if with_back:
-                    mv_ref[phase, me, pl.ds(r * tiles_row + t, 1), :] = jnp.sum(tile * down, axis=0, keepdims=True)
-            mv_ref[phase, me, pl.ds(tiles_all + r, 1), :] = jnp.sum(total.T, axis=0, keepdims=True)
-            return carry
-
-        lax.fori_loop(0, rows, row, 0)
+                    line = r * tiles_row + t
+                    mv_ref[phase, me, line : line + 1, :] = jnp.sum(tile * down, axis=0, keepdims=True)
+            mv_ref[phase, me, tiles_all + r : tiles_all + r + 1, :] = jnp.sum(total.T, axis=0, keepdims=True)
+            if with_back and (r + 1) * tiles_row == half:
+                send_lines(phase, 0, half)
 
     def start_matvec(phase, vector):
         vector_ref[phase] = vector
         products(phase, True)
-        spread_to_frac(mv_ref.at[phase, me], mv_ref.at[phase], mv_send.at[phase], mv_recv.at[phase])
+        send_lines(phase, half, lines_mv)
+        sent.append((mv_ref.at[phase, pl.ds(0, n_frac - 1)], mv_send.at[phase]))
 
     def finish_matvec(phase, vector):
         take(mv_ref.at[phase, pl.ds(0, n_frac - 1)], mv_recv.at[phase])
         forward = mv_ref[phase, :, tiles_all:].reshape(blocks, size_b)
         product = total_of(vector * (diag * vector + forward))
         arrived = mv_ref[phase].reshape(n_frac * lines_mv, size_b)
-        both = sum(dot_nn(targets, part) for part in split_parts(arrived, 3))
+        both = sum(dot_nn(targets, part) for part in split_parts(arrived, 2))
         return product, diag * vector + 0.5 * both
 
     def set_row_hot():
@@ -359,6 +373,7 @@
 
     tiles_copy.wait()
     start_matvec(0, begin)
+    set_inverse()
     set_row_hot()
     msource_copy.wait()
     set_sources(flux)
@@ -401,12 +416,7 @@
             send_halo(3)
         elif number == 4:
             wait_halo(3)
-            for q in range(4):
-                part = pl.ds(q * part_x, part_x)
-                sweep_part(3, q * part_x, (q + 1) * part_x)
-                copy = pltpu.make_async_copy(result_ref.at[part], out_hbm.at[part], out_sem.at[q])
-                copy.start()
-                results.append(copy)
+            sweep_part(3, 0, width_x)
         elif number == 5:
             take(back_in_ref.at[pl.ds(0, devices - 1)], back_recv)
             came = back_in_ref[...].reshape(devices, LANES)
@@ -418,7 +428,6 @@
             flux_out_ref[...] = jnp.sum(jnp.where(spot == want, lines_back, 0.0), axis=0, keepdims=True)
 
     state = {}
-    results = []
     last = OUTER * CG_ITERS - 1
     for number in range(OUTER * CG_ITERS):
         step = number % CG_ITERS
@@ -470,8 +479,6 @@
         take(ref, sem)
     for copy in slow_sends:
         copy.wait_send()
-    for copy in results:
-        copy.wait()
 
 
 def coupled(pressure, face, cell_coef, matrix_source, tiles, owner, cells, places, kappa, tile_cols, diag, begin, fsource):
@@ -489,23 +496,22 @@
     f32, bf16 = jnp.float32, jnp.bfloat16
     vmem = pl.BlockSpec(memory_space=pltpu.VMEM)
     smem = pl.BlockSpec(memory_space=pltpu.SMEM)
-    hbm = pl.BlockSpec(memory_space=pl.ANY)
+    hbm = pl.BlockSpec(memory_space=pltpu.HBM)
     phases = OUTER * CG_ITERS + 1
     sweeps = OUTER * SWEEPS
     dma = pltpu.SemaphoreType.DMA
     return pl.pallas_call(
         functools.partial(coupled_kernel, n_frac, n_mat),
         out_shape=(
-            jax.ShapeDtypeStruct((x, y, z), f32),
-            jax.ShapeDtypeStruct((rows, size_b), f32),
-            jax.ShapeDtypeStruct((1, mortars), f32),
+            pltpu.VMEM((x, y, z), f32),
+            pltpu.VMEM((rows, size_b), f32),
+            pltpu.VMEM((1, mortars), f32),
         ),
         in_specs=[hbm] * 5 + [vmem] * 4 + [smem] + [vmem] * 3,
-        out_specs=(hbm, vmem, vmem),
+        out_specs=(vmem, vmem, vmem),
         scratch_shapes=[
             pltpu.VMEM((sweeps, x + 2, y, z), f32),
             pltpu.VMEM((x + 1, y, z), f32),
-            pltpu.VMEM((x, y, z), f32),
             pltpu.VMEM((x, y, z), f32),
             pltpu.VMEM((x, y, z), f32),
             pltpu.VMEM((x, y, z), f32),
@@ -538,7 +544,6 @@
             pltpu.VMEM((groups, 1, LANES), f32),
             pltpu.VMEM((devices, 1, LANES), f32),
             dma((7,)),
-            dma((4,)),
             dma,
             dma,
             dma((4,)),

time: 71 us -> 62.2 us (0.88)
  Pallas kernels: 65.4 us -> 59.2 us
  local copies, waits for them, and re-layouts: 4.8 us -> 2.14 us
    pallas_call x1, Pallas kernels: 65.4 us -> 59.2 us  [coupled(): pl.pallas_call(functools.partial(coupled_kernel, n_frac, n_mat), out_shap...]
    unnamed x3, local copies, waits for them, and re-layouts: 4.8 us -> 2.14 us
where the time goes in v2:
time: 62.2 us; the launch traced here: 62 us
  Pallas kernels  59.2 us (95%)
  local copies, waits for them, and re-layouts  2.14 us (3%)
  between operations  0.65 us (1%)
    pallas_call x1, Pallas kernels, coupled(): pl.pallas_call(functools.partial(coupled_kernel, n_frac, n_mat), out_shap...  59.2 us
    unnamed x3, local copies, waits for them, and re-layouts  2.14 us

profile of v2, /device:TPU:0, one launch (start us, length us, event | category | flops | bytes accessed | tf_op | source)
XLA Modules:
  0.0 62.0 jit_solution(9383996791029276321)
XLA Ops:
  0.6 59.2 %coupled.1 = (f32[16,64,256]{2,1,0:T(8,128)S(1)}, f32[8,128]{1,0:T(8,128)S(1)}, f32[1,512]{1,0:T(1,128)S(1)}) custom-call(f32[16,64,256]{2,1,0:T(8,128)} %refs_0_.1, f32[3,16,64,256]{3,2,1,0:T(8,128)} %refs_1_.1, f32[16,64,256]{2,1,0:T(8,128)} %refs_2_.1, f32[16,64,256]{2,1,0:T(8,128)} %refs_3_.1, f32[8,4,128,128]{3,2,1,0:T(8,128)} %refs_4_.1, ...), custom_call_target="tpu_custom_call" | custom-call | tf_op jit(solution)/shard_map/coupled/pallas_call | solution.py:503
  59.9 1.0 %copy.19 = f32[16,64,256]{2,1,0:T(8,128)} copy(f32[16,64,256]{2,1,0:T(8,128)S(1)} %get-tuple-element.9) | data formatting | bytes 2097152
  60.9 0.6 copy.20
  61.4 0.6 copy.21

commit v3 on v2

--- a/solution.py
+++ b/solution.py
@@ -50,7 +50,7 @@
      row_hot_ref, lane_hot_ref, side_ref, edge_ref, ty_edge_ref, ty_side_ref, mort_out_ref, mort_in_ref, vec_ref,
      dest_out_ref, dest_in_ref, mv_ref, vector_ref, rs_out_0, rs_in_0, ag_0, rs_out_1, rs_in_1, ag_1, part_out_ref, part_in_ref,
      back_out_ref, back_in_ref, local_sem, mort_send, mort_recv, vec_send, vec_recv, mv_send, mv_recv,
-     rs_send, rs_recv, ag_send, ag_recv, part_send, part_recv, back_send, back_recv, halo_send, halo_recv) = scratch
+     pair_recv, rs_send, rs_recv, ag_send, ag_recv, part_send, part_recv, back_send, back_recv, halo_send, halo_recv) = scratch
     rows, tiles_row, size_b = tiles_ref.shape[0], tiles_ref.shape[1], tiles_ref.shape[3]
     width_x, width_y, depth_z = inv_ref.shape
     grid_rows = width_x * width_y
@@ -61,14 +61,17 @@
     groups = devices // per
     slots = devices * capacity
     blocks = rows * n_frac
-    tiles_all = rows * tiles_row
-    lines_mv = tiles_all + rows
+    half = rows // 2
+    lines_half = half * tiles_row + half
+    stride = -(-lines_half // 8) * 8
     share = blocks // devices
     sweeps = OUTER * SWEEPS
     f32, i32 = jnp.float32, jnp.int32
     me = lax.axis_index("frac")
     me_mat = lax.axis_index("mat")
     me_dev = me_mat * n_frac + me
+    core = lax.rem(me_mat, 2)
+    sibling = me_mat + 1 - 2 * core
     everyone = [(c, k) for c in range(n_mat) for k in range(n_frac) if c or k]
 
     barrier = pltpu.get_barrier_semaphore()
@@ -130,11 +133,16 @@
     mort_out_ref[...] = outgoing.reshape(devices, 1, LANES)
 
     lane_line = lax.broadcasted_iota(i32, (1, LANES), 1)
-    target_row = jnp.where((lane_line >= tiles_all) & (lane_line < lines_mv), me * rows + lane_line - tiles_all, -1)
-    for r in range(rows):
-        for t in range(tiles_row):
-            target_row = jnp.where(lane_line == r * tiles_row + t, cols_ref[t, r], target_row)
+    target_row = jnp.full((1, LANES), -1, i32)
+    for h in range(2):
+        for n in range(lines_half):
+            r, t = h * half + n // tiles_row, n % tiles_row
+            block = cols_ref[t, r] if n < half * tiles_row else me * rows + h * half + n - half * tiles_row
+            target_row = jnp.where(lane_line == h * stride + n, block, target_row)
     dest_out_ref[...] = target_row.astype(f32)
+
+    if stride > lines_half:
+        mv_ref[:, :, :, lines_half:, :] = jnp.zeros((mv_ref.shape[0], n_frac, 2, stride - lines_half, size_b), f32)
 
     pl.semaphore_wait(barrier, devices - 1)
     spread_to_all(lambda target: mort_out_ref.at[target], mort_in_ref, mort_send, mort_recv)
@@ -306,46 +314,48 @@
         take(whole.at[pl.ds(0, devices - 1)], ag_recv.at[stage])
         return [whole[:, n].reshape(blocks, size_b) for n in range(whole.shape[1])]
 
-    half = tiles_all // 2
-
-    def send_lines(phase, low, high):
-        part = pl.ds(low, high - low)
-        for k in range(1, n_frac):
-            send(
-                mv_ref.at[phase, me, part],
-                mv_ref.at[phase, me, part],
-                mv_send.at[phase],
-                mv_recv.at[phase],
-                {"frac": lax.rem(me + k, n_frac)},
-            )
-
-    def products(phase, with_back):
-        own = vector_ref[phase, pl.ds(pl.multiple_of(me * rows, rows), rows), :]
-        for r in range(rows):
-            down = jnp.broadcast_to(own[r : r + 1], (size_b, size_b)).T
-            total = None
-            for t in range(tiles_row):
-                tile = tiles_ref[r, t]
-                part = tile * vector_ref[phase, pl.ds(cols_ref[t, r], 1), :]
-                total = part if total is None else total + part
-                if with_back:
-                    line = r * tiles_row + t
-                    mv_ref[phase, me, line : line + 1, :] = jnp.sum(tile * down, axis=0, keepdims=True)
-            mv_ref[phase, me, tiles_all + r : tiles_all + r + 1, :] = jnp.sum(total.T, axis=0, keepdims=True)
-            if with_back and (r + 1) * tiles_row == half:
-                send_lines(phase, 0, half)
+    def tile_line(phase, r, down, place):
+        total = None
+        for t in range(tiles_row):
+            tile = tiles_ref[r, t]
+            part = tile * vector_ref[phase, pl.ds(cols_ref[t, r], 1), :]
+            total = part if total is None else total + part
+            if place is not None:
+                line = place * tiles_row + t
+                mv_ref[phase, me, core, line : line + 1, :] = jnp.sum(tile * down, axis=0, keepdims=True)
+        return jnp.sum(total.T, axis=0, keepdims=True)
+
+    falling = [n_frac - 1 - n - (n_frac - 1 - n <= me).astype(i32) for n in range(n_frac - 1)]
+    rising = [n + (n >= me).astype(i32) for n in range(n_frac - 1)]
+    near_first = [jnp.where(2 * me < n_frac, up, down) for up, down in zip(rising, falling)]
+    lines_sent = pl.ds(0, lines_half)
 
     def start_matvec(phase, vector):
         vector_ref[phase] = vector
-        products(phase, True)
-        send_lines(phase, half, lines_mv)
-        sent.append((mv_ref.at[phase, pl.ds(0, n_frac - 1)], mv_send.at[phase]))
+        for n in range(half):
+            r = core * half + n
+            own = vector_ref[phase, pl.ds(me * rows + r, 1), :]
+            forward = tile_line(phase, r, jnp.broadcast_to(own, (size_b, size_b)).T, n)
+            line = half * tiles_row + n
+            mv_ref[phase, me, core, line : line + 1, :] = forward
+        lines = mv_ref.at[phase, me, core, lines_sent]
+        for target in reversed(near_first):
+            send(lines, lines, mv_send.at[phase], mv_recv.at[phase, me], {"frac": target})
+        send(lines, lines, mv_send.at[phase], pair_recv.at[phase], {"mat": sibling})
+        sent.append((mv_ref.at[phase, :, 0, lines_sent], mv_send.at[phase]))
+        sent.append((mv_ref.at[phase, pl.ds(0, n_frac - 1), 0, lines_sent], mv_send.at[phase]))
+
+    def pass_on(phase):
+        for source in near_first:
+            lines = mv_ref.at[phase, source, core, lines_sent]
+            take(lines, mv_recv.at[phase, source])
+            send(lines, lines, mv_send.at[phase], pair_recv.at[phase], {"mat": sibling})
 
     def finish_matvec(phase, vector):
-        take(mv_ref.at[phase, pl.ds(0, n_frac - 1)], mv_recv.at[phase])
-        forward = mv_ref[phase, :, tiles_all:].reshape(blocks, size_b)
+        take(mv_ref.at[phase, :, 0, lines_sent], pair_recv.at[phase])
+        forward = mv_ref[phase, :, :, half * tiles_row : lines_half].reshape(blocks, size_b)
         product = total_of(vector * (diag * vector + forward))
-        arrived = mv_ref[phase].reshape(n_frac * lines_mv, size_b)
+        arrived = mv_ref[phase].reshape(n_frac * 2 * stride, size_b)
         both = sum(dot_nn(targets, part) for part in split_parts(arrived, 2))
         return product, diag * vector + 0.5 * both
 
@@ -380,11 +390,12 @@
     take(dest_in_ref.at[pl.ds(0, n_frac - 1)], vec_recv.at[3])
     block_line = lax.broadcasted_iota(i32, (blocks, LANES), 0)
     targets = jnp.concatenate(
-        [as_hot(block_line == dest_in_ref[d].astype(i32))[:, :lines_mv] for d in range(n_frac)], axis=1
+        [as_hot(block_line == dest_in_ref[d].astype(i32))[:, : 2 * stride] for d in range(n_frac)], axis=1
     )
     fsource = gathered(1)
     diag = gathered(2)
     gather_share(0)
+    pass_on(0)
 
     wait_halo(0)
     sweep_part(0, 0, width_x)
@@ -400,21 +411,24 @@
             sweep_part(1, 0, width_x)
             send_halo(2)
             set_parts(2)
+            state["weight"] = landed(kappa)
+        elif number == 1:
             state["trace"] = traces()
-            scatter_share(1, [landed(kappa * state["trace"]), landed(kappa)])
+            scatter_share(1, [landed(kappa * state["trace"]), state["weight"]])
         elif number == 2:
             gather_share(1)
         elif number == 3:
             flux = kappa * (state["trace"] - at_slots(state["fracture"]))
-            for g in range(groups):
-                back_out_ref[g] = flux[:, g * LANES : (g + 1) * LANES]
-            spread_to_all(lambda target: back_out_ref.at[target // per], back_in_ref, back_send, back_recv)
-            back_in_ref[me_dev] = back_out_ref[me_dev // per]
+            state["flux"] = flux
             set_sources(flux)
             wait_halo(2)
             sweep_part(2, 0, width_x)
             send_halo(3)
         elif number == 4:
+            for g in range(groups):
+                back_out_ref[g] = state["flux"][:, g * LANES : (g + 1) * LANES]
+            spread_to_all(lambda target: back_out_ref.at[target // per], back_in_ref, back_send, back_recv)
+            back_in_ref[me_dev] = back_out_ref[me_dev // per]
             wait_halo(3)
             sweep_part(3, 0, width_x)
         elif number == 5:
@@ -440,16 +454,17 @@
             start_matvec(phase, residual)
         else:
             vector_ref[phase] = residual
-            products(phase, False)
-            mine = pl.ds(pl.multiple_of(me * rows, rows), rows)
-            part_out_ref[...] = jnp.sum(
-                vector_ref[phase, mine, :] * mv_ref[phase, me, tiles_all:, :], axis=0, keepdims=True
-            )
+            partial = jnp.zeros((1, size_b), f32)
+            for r in range(rows):
+                own = vector_ref[phase, pl.ds(me * rows + r, 1), :]
+                partial = partial + own * tile_line(phase, r, None, None)
+            part_out_ref[...] = partial
             spread_to_frac(part_out_ref, part_in_ref, part_send, part_recv)
             part_in_ref[me] = part_out_ref[...]
         norm_next = total_of(residual * residual)
         fill(number)
         if number < last:
+            pass_on(phase)
             product, image = finish_matvec(phase, residual)
         else:
             take(part_in_ref.at[pl.ds(0, n_frac - 1)], part_recv)
@@ -492,7 +507,7 @@
     slots = devices * capacity
     groups = slots // LANES
     share = blocks // devices
-    lines_mv = rows * tiles_row + rows
+    stride = -(-(rows // 2 * (tiles_row + 1)) // 8) * 8
     f32, bf16 = jnp.float32, jnp.bfloat16
     vmem = pl.BlockSpec(memory_space=pltpu.VMEM)
     smem = pl.BlockSpec(memory_space=pltpu.SMEM)
@@ -531,7 +546,7 @@
             pltpu.VMEM((3, n_frac, rows, size_b), f32),
             pltpu.VMEM((1, LANES), f32),
             pltpu.VMEM((n_frac, 1, LANES), f32),
-            pltpu.VMEM((phases, n_frac, lines_mv, size_b), f32),
+            pltpu.VMEM((phases, n_frac, 2, stride, size_b), f32),
             pltpu.VMEM((phases, blocks, size_b), f32),
             pltpu.VMEM((devices, 1, share, size_b), f32),
             pltpu.VMEM((devices, 1, share, size_b), f32),
@@ -549,6 +564,7 @@
             dma((4,)),
             dma((4,)),
             dma((phases,)),
+            dma((phases, n_frac)),
             dma((phases,)),
             dma((2,)),
             dma((2,)),

time: 62.2 us -> 60.2 us (0.968)
  Pallas kernels: 59.2 us -> 57.2 us
    pallas_call x1, Pallas kernels: 59.2 us -> 57.2 us  [coupled(): pl.pallas_call(functools.partial(coupled_kernel, n_frac, n_mat), out_shap...]
where the time goes in v3:
time: 60.2 us; the launch traced here: 60 us
  Pallas kernels  57.2 us (95%)
  local copies, waits for them, and re-layouts  2.14 us (4%)
  between operations  0.64 us (1%)
    pallas_call x1, Pallas kernels, coupled(): pl.pallas_call(functools.partial(coupled_kernel, n_frac, n_mat), out_shap...  57.2 us
    unnamed x3, local copies, waits for them, and re-layouts  2.14 us

profile of v3, /device:TPU:0, one launch (start us, length us, event | category | flops | bytes accessed | tf_op | source)
XLA Modules:
  0.0 60.0 jit_solution(15747427452570185203)
XLA Ops:
  0.6 57.2 %coupled.1 = (f32[16,64,256]{2,1,0:T(8,128)S(1)}, f32[8,128]{1,0:T(8,128)S(1)}, f32[1,512]{1,0:T(1,128)S(1)}) custom-call(f32[16,64,256]{2,1,0:T(8,128)} %refs_0_.1, f32[3,16,64,256]{3,2,1,0:T(8,128)} %refs_1_.1, f32[16,64,256]{2,1,0:T(8,128)} %refs_2_.1, f32[16,64,256]{2,1,0:T(8,128)} %refs_3_.1, f32[8,4,128,128]{3,2,1,0:T(8,128)} %refs_4_.1, ...), custom_call_target="tpu_custom_call" | custom-call | tf_op jit(solution)/shard_map/coupled/pallas_call | solution.py:518
  57.9 1.0 %copy.19 = f32[16,64,256]{2,1,0:T(8,128)} copy(f32[16,64,256]{2,1,0:T(8,128)S(1)} %get-tuple-element.9) | data formatting | bytes 2097152
  58.8 0.6 copy.20
  59.4 0.6 copy.21

commit v4 on v3

--- a/solution.py
+++ b/solution.py
@@ -44,9 +44,9 @@
 
 
 def coupled_kernel(n_frac, n_mat, *refs):
-    (press_hbm, face_hbm, cell_hbm, msource_hbm, tiles_hbm, owner_ref, cells_ref, places_ref, kappa_in_ref, cols_ref,
-     diag_ref, begin_ref, fsource_ref, out_ref, own_ref, flux_out_ref, *scratch) = refs
-    (grid_ref, tx_ref, ty_ref, tz_ref, inv_ref, cell_ref, msource_ref, base_ref, tiles_ref, parts_ref,
+    (press_hbm, face_hbm, cell_hbm, msource_hbm, tiles_hbm, owner_hbm, cells_hbm, places_hbm, kappa_hbm, cols_hbm,
+     diag_hbm, begin_hbm, fsource_hbm, out_ref, own_ref, flux_out_ref, *scratch) = refs
+    (owner_ref, cells_ref, places_ref, kappa_in_ref, cols_ref, diag_ref, begin_ref, fsource_ref, targets_ref, grid_ref, tx_ref, ty_ref, tz_ref, inv_ref, cell_ref, msource_ref, base_ref, tiles_ref, parts_ref,
      row_hot_ref, lane_hot_ref, side_ref, edge_ref, ty_edge_ref, ty_side_ref, mort_out_ref, mort_in_ref, vec_ref,
      dest_out_ref, dest_in_ref, mv_ref, vector_ref, rs_out_0, rs_in_0, ag_0, rs_out_1, rs_in_1, ag_1, part_out_ref, part_in_ref,
      back_out_ref, back_in_ref, local_sem, mort_send, mort_recv, vec_send, vec_recv, mv_send, mv_recv,
@@ -88,6 +88,16 @@
         copy.start()
         return copy
 
+    small_copies = [
+        load(7, owner_hbm, owner_ref),
+        load(8, cells_hbm, cells_ref),
+        load(9, places_hbm, places_ref),
+        load(10, kappa_hbm, kappa_in_ref),
+        load(11, cols_hbm, cols_ref),
+        load(12, begin_hbm, begin_ref),
+        load(13, fsource_hbm, fsource_ref),
+        load(14, diag_hbm, diag_ref),
+    ]
     press_copy = load(0, press_hbm, grid_ref.at[0, pl.ds(1, width_x)])
     tx_copy = load(1, face_hbm.at[0], tx_ref.at[pl.ds(1, width_x)])
     ty_copy = load(2, face_hbm.at[1], ty_ref)
@@ -119,6 +129,8 @@
             send(source, landing.at[me], send_sem, recv_sem, {"frac": lax.rem(me + k, n_frac)})
         sent.append((landing.at[pl.ds(0, n_frac - 1)], send_sem))
 
+    for copy in small_copies:
+        copy.wait()
     owner = owner_ref[...]
     named = lax.broadcasted_iota(i32, (devices, mortars), 0) == owner
     named_hot = as_hot(named)
@@ -351,13 +363,16 @@
             take(lines, mv_recv.at[phase, source])
             send(lines, lines, mv_send.at[phase], pair_recv.at[phase], {"mat": sibling})
 
+    def combined(phase, side):
+        arrived = mv_ref[phase, :, side].reshape(n_frac * stride, size_b)
+        return sum(dot_nn(targets_ref[side], part) for part in split_parts(arrived, 2))
+
     def finish_matvec(phase, vector):
+        direct = combined(phase, core)
         take(mv_ref.at[phase, :, 0, lines_sent], pair_recv.at[phase])
         forward = mv_ref[phase, :, :, half * tiles_row : lines_half].reshape(blocks, size_b)
         product = total_of(vector * (diag * vector + forward))
-        arrived = mv_ref[phase].reshape(n_frac * 2 * stride, size_b)
-        both = sum(dot_nn(targets, part) for part in split_parts(arrived, 2))
-        return product, diag * vector + 0.5 * both
+        return product, diag * vector + 0.5 * (direct + combined(phase, 1 - core))
 
     def set_row_hot():
         line = lax.broadcasted_iota(i32, (grid_rows, quarter), 0)
@@ -389,9 +404,9 @@
     set_sources(flux)
     take(dest_in_ref.at[pl.ds(0, n_frac - 1)], vec_recv.at[3])
     block_line = lax.broadcasted_iota(i32, (blocks, LANES), 0)
-    targets = jnp.concatenate(
-        [as_hot(block_line == dest_in_ref[d].astype(i32))[:, : 2 * stride] for d in range(n_frac)], axis=1
-    )
+    hots = [as_hot(block_line == dest_in_ref[d].astype(i32)) for d in range(n_frac)]
+    for h in range(2):
+        targets_ref[h] = jnp.concatenate([hot[:, h * stride : (h + 1) * stride] for hot in hots], axis=1)
     fsource = gathered(1)
     diag = gathered(2)
     gather_share(0)
@@ -510,7 +525,6 @@
     stride = -(-(rows // 2 * (tiles_row + 1)) // 8) * 8
     f32, bf16 = jnp.float32, jnp.bfloat16
     vmem = pl.BlockSpec(memory_space=pltpu.VMEM)
-    smem = pl.BlockSpec(memory_space=pltpu.SMEM)
     hbm = pl.BlockSpec(memory_space=pltpu.HBM)
     phases = OUTER * CG_ITERS + 1
     sweeps = OUTER * SWEEPS
@@ -522,9 +536,18 @@
             pltpu.VMEM((rows, size_b), f32),
             pltpu.VMEM((1, mortars), f32),
         ),
-        in_specs=[hbm] * 5 + [vmem] * 4 + [smem] + [vmem] * 3,
+        in_specs=[hbm] * 13,
         out_specs=(vmem, vmem, vmem),
         scratch_shapes=[
+            pltpu.VMEM((1, mortars), jnp.int32),
+            pltpu.VMEM((1, mortars), jnp.int32),
+            pltpu.VMEM((1, mortars), jnp.int32),
+            pltpu.VMEM((1, mortars), f32),
+            pltpu.SMEM((tiles_row, rows), jnp.int32),
+            pltpu.VMEM((rows, size_b), f32),
+            pltpu.VMEM((rows, size_b), f32),
+            pltpu.VMEM((rows, size_b), f32),
+            pltpu.VMEM((2, blocks, n_frac * stride), bf16),
             pltpu.VMEM((sweeps, x + 2, y, z), f32),
             pltpu.VMEM((x + 1, y, z), f32),
             pltpu.VMEM((x, y, z), f32),
@@ -558,7 +581,7 @@
             pltpu.VMEM((n_frac, 1, size_b), f32),
             pltpu.VMEM((groups, 1, LANES), f32),
             pltpu.VMEM((devices, 1, LANES), f32),
-            dma((7,)),
+            dma((15,)),
             dma,
             dma,
             dma((4,)),

time: 60.2 us -> 59.3 us (0.985)
  Pallas kernels: 57.2 us -> 56.1 us
    pallas_call x1, Pallas kernels: 57.2 us -> 56.1 us  [coupled(): pl.pallas_call(functools.partial(coupled_kernel, n_frac, n_mat), out_shap...]
where the time goes in v4:
time: 59.3 us; the launch traced here: 58.9 us
  Pallas kernels  56.1 us (95%)
  local copies, waits for them, and re-layouts  2.14 us (4%)
  between operations  0.64 us (1%)
    pallas_call x1, Pallas kernels, coupled(): pl.pallas_call(functools.partial(coupled_kernel, n_frac, n_mat), out_shap...  56.1 us
    unnamed x3, local copies, waits for them, and re-layouts  2.14 us

profile of v4, /device:TPU:0, one launch (start us, length us, event | category | flops | bytes accessed | tf_op | source)
XLA Modules:
  0.0 58.9 jit_solution(11482070510539529354)
XLA Ops:
  0.6 56.1 %coupled.1 = (f32[16,64,256]{2,1,0:T(8,128)S(1)}, f32[8,128]{1,0:T(8,128)S(1)}, f32[1,512]{1,0:T(1,128)S(1)}) custom-call(f32[16,64,256]{2,1,0:T(8,128)} %refs_0_.1, f32[3,16,64,256]{3,2,1,0:T(8,128)} %refs_1_.1, f32[16,64,256]{2,1,0:T(8,128)} %refs_2_.1, f32[16,64,256]{2,1,0:T(8,128)} %refs_3_.1, f32[8,4,128,128]{3,2,1,0:T(8,128)} %refs_4_.1, ...), custom_call_target="tpu_custom_call" | custom-call | tf_op jit(solution)/shard_map/coupled/pallas_call | solution.py:532
  56.7 1.0 %copy.19 = f32[16,64,256]{2,1,0:T(8,128)} copy(f32[16,64,256]{2,1,0:T(8,128)S(1)} %get-tuple-element.9) | data formatting | bytes 2097152
  57.7 0.6 %copy.20 = f32[1024]{0:T(1024)} copy(f32[1024]{0:T(1024)S(1)} %bitcast.10) | data formatting | bytes 8192
  58.3 0.6 copy.21

commit v5 on v4

--- a/solution.py
+++ b/solution.py
@@ -121,13 +121,30 @@
     def spread_to_all(source, landing, send_sem, recv_sem):
         for c, k in everyone:
             mat, frac = lax.rem(me_mat + c, n_mat), lax.rem(me + k, n_frac)
-            send(source(mat * n_frac + frac), landing.at[me_dev], send_sem, recv_sem, {"mat": mat, "frac": frac})
+            arrival = recv_sem(frac) if callable(recv_sem) else recv_sem
+            send(source(mat * n_frac + frac), landing.at[me_dev], send_sem, arrival, {"mat": mat, "frac": frac})
         sent.append((landing.at[pl.ds(0, devices - 1)], send_sem))
 
     def spread_to_frac(source, landing, send_sem, recv_sem):
         for k in range(1, n_frac):
             send(source, landing.at[me], send_sem, recv_sem, {"frac": lax.rem(me + k, n_frac)})
         sent.append((landing.at[pl.ds(0, n_frac - 1)], send_sem))
+
+    sides = 2 if n_frac == 2 * per else 1
+    my_side = me // per if sides == 2 else 0
+
+    def side_from_here(frac):
+        return lax.rem(frac // per + my_side, 2) if sides == 2 else 0
+
+    def group_at(position):
+        if sides == 1:
+            return position
+        return 2 * (position % n_mat) + lax.rem(my_side + position // n_mat, 2)
+
+    def position_of(group):
+        if sides == 1:
+            return group
+        return group // 2 + n_mat * lax.rem(lax.rem(group, 2) + my_side, 2)
 
     for copy in small_copies:
         copy.wait()
@@ -157,7 +174,7 @@
         mv_ref[:, :, :, lines_half:, :] = jnp.zeros((mv_ref.shape[0], n_frac, 2, stride - lines_half, size_b), f32)
 
     pl.semaphore_wait(barrier, devices - 1)
-    spread_to_all(lambda target: mort_out_ref.at[target], mort_in_ref, mort_send, mort_recv)
+    spread_to_all(lambda target: mort_out_ref.at[target], mort_in_ref, mort_send, lambda frac: mort_recv.at[side_from_here(frac)])
     mort_in_ref[me_dev] = mort_out_ref[me_dev]
     spread_to_frac(begin_ref, vec_ref.at[0], vec_send.at[0], vec_recv.at[0])
     spread_to_frac(dest_out_ref, dest_in_ref, vec_send.at[3], vec_recv.at[3])
@@ -260,41 +277,59 @@
 
     set_parts(0)
 
-    take(mort_in_ref.at[pl.ds(0, devices - 1)], mort_recv)
-    arrived = mort_in_ref[...].reshape(devices, LANES)
-    window = lax.broadcasted_iota(i32, (devices, LANES), 1) // capacity
-    device = lax.broadcasted_iota(i32, (devices, LANES), 0)
-
-    def slot_line(word_no):
-        turned = pltpu.roll(arrived, LANES - word_no * capacity, 1) if word_no else arrived
-        chosen = jnp.where(lax.rem(device, per) == window, turned, 0.0)
-        return jnp.concatenate(
-            [jnp.sum(chosen[g * per : (g + 1) * per], axis=0, keepdims=True) for g in range(groups)], axis=1
+    window = lax.broadcasted_iota(i32, (per, LANES), 1) // capacity
+    device = lax.broadcasted_iota(i32, (per, LANES), 0)
+    quarter = slots // 4
+    grid_line = lax.broadcasted_iota(i32, (grid_rows, quarter), 0)
+
+    def slot_lines(low, high):
+        words = [[], [], []]
+        for position in range(low, high):
+            arrived = mort_in_ref[pl.ds(group_at(position) * per, per)].reshape(per, LANES)
+            for n in range(3):
+                turned = pltpu.roll(arrived, LANES - n * capacity, 1) if n else arrived
+                words[n].append(jnp.sum(jnp.where(device == window, turned, 0.0), axis=0, keepdims=True))
+        return [jnp.concatenate(word, axis=1) for word in words]
+
+    def set_lane_hot(low, cells_here):
+        row = cells_here // depth_z
+        width = row.shape[1]
+        lane_hot_ref[:, low : low + width] = as_hot(
+            lax.broadcasted_iota(i32, (depth_z, width), 0) == cells_here - row * depth_z
         )
-
-    cell = slot_line(0).astype(i32)
-    place = slot_line(1).astype(i32)
-    kappa = slot_line(2)
-    cell_row = cell // depth_z
-    cell_lane = cell - cell_row * depth_z
+        return row
+
+    def trace_quarter(q, rows_here):
+        hot = lane_hot_ref[:, q * quarter : (q + 1) * quarter]
+        picked = dot_nn(parts_ref[0], hot) + dot_nn(parts_ref[1], hot)
+        return jnp.sum(jnp.where(grid_line == rows_here, picked, 0.0), axis=0, keepdims=True)
+
+    found, row_list, place_list, kappa_list = [], [], [], []
+    per_quarter = quarter // LANES
+    for side in range(sides):
+        count = devices // sides - (1 if side == 0 else 0)
+        take(mort_in_ref.at[pl.ds(0, count)], mort_recv.at[side])
+        first, last_group = side * groups // sides, (side + 1) * groups // sides
+        cell_words, place_words, kappa_words = slot_lines(first, last_group)
+        rows_here = set_lane_hot(first * LANES, cell_words.astype(i32))
+        row_list.append(rows_here)
+        place_list.append(place_words)
+        kappa_list.append(kappa_words)
+        for q in range(first // per_quarter, last_group // per_quarter):
+            cut = q * quarter - first * LANES
+            found.append(trace_quarter(q, rows_here[:, cut : cut + quarter]))
+    cell_row = jnp.concatenate(row_list, axis=1)
+    place = jnp.concatenate(place_list, axis=1).astype(i32)
+    kappa = jnp.concatenate(kappa_list, axis=1)
     block_of = place // size_b
     lane_of = place - block_of * size_b
-    lane_hot_ref[...] = as_hot(lax.broadcasted_iota(i32, (depth_z, slots), 0) == cell_lane)
     by_lane = as_hot(lax.broadcasted_iota(i32, (size_b, slots), 0) == lane_of)
     by_block = lax.broadcasted_iota(i32, (blocks, slots), 0) == block_of
 
-    quarter = slots // 4
-    grid_line = lax.broadcasted_iota(i32, (grid_rows, quarter), 0)
-
     def traces():
-        found = []
-        for q in range(4):
-            hot = lane_hot_ref[:, q * quarter : (q + 1) * quarter]
-            picked = dot_nn(parts_ref[0], hot) + dot_nn(parts_ref[1], hot)
-            found.append(
-                jnp.sum(jnp.where(grid_line == cell_row[:, q * quarter : (q + 1) * quarter], picked, 0.0), axis=0, keepdims=True)
-            )
-        return jnp.concatenate(found, axis=1)
+        return jnp.concatenate(
+            [trace_quarter(q, cell_row[:, q * quarter : (q + 1) * quarter]) for q in range(4)], axis=1
+        )
 
     def at_slots(values):
         picked = sum(dot_nn(part, by_lane) for part in split_parts(values, 3))
@@ -392,7 +427,7 @@
             base_ref[low : low + part_x] = msource_ref[low : low + part_x] + total.reshape(part_x, width_y, depth_z)
 
     begin = gathered(0)
-    trace = traces()
+    trace = jnp.concatenate(found, axis=1)
     flux = kappa * (trace - at_slots(begin))
     scatter_share(0, [landed(flux)])
 
@@ -442,8 +477,8 @@
         elif number == 4:
             for g in range(groups):
                 back_out_ref[g] = state["flux"][:, g * LANES : (g + 1) * LANES]
-            spread_to_all(lambda target: back_out_ref.at[target // per], back_in_ref, back_send, back_recv)
-            back_in_ref[me_dev] = back_out_ref[me_dev // per]
+            spread_to_all(lambda target: back_out_ref.at[position_of(target // per)], back_in_ref, back_send, back_recv)
+            back_in_ref[me_dev] = back_out_ref[position_of(me_dev // per)]
             wait_halo(3)
             sweep_part(3, 0, width_x)
         elif number == 5:
@@ -583,7 +618,7 @@
             pltpu.VMEM((devices, 1, LANES), f32),
             dma((15,)),
             dma,
-            dma,
+            dma((2,)),
             dma((4,)),
             dma((4,)),
             dma((phases,)),

time: 59.3 us -> 58.5 us (0.987)
  no operation moved by 1% of the time
where the time goes in v5:
time: 58.5 us; the launch traced here: 58.4 us
  Pallas kernels  55.6 us (95%)
  local copies, waits for them, and re-layouts  2.14 us (4%)
  between operations  0.65 us (1%)
    pallas_call x1, Pallas kernels, coupled(): pl.pallas_call(functools.partial(coupled_kernel, n_frac, n_mat), out_shap...  55.6 us
    unnamed x3, local copies, waits for them, and re-layouts  2.14 us

profile of v5, /device:TPU:0, one launch (start us, length us, event | category | flops | bytes accessed | tf_op | source)
XLA Modules:
  0.0 58.4 jit_solution(4751603561418072387)
XLA Ops:
  0.6 55.6 %coupled.1 = (f32[16,64,256]{2,1,0:T(8,128)S(1)}, f32[8,128]{1,0:T(8,128)S(1)}, f32[1,512]{1,0:T(1,128)S(1)}) custom-call(f32[16,64,256]{2,1,0:T(8,128)} %refs_0_.1, f32[3,16,64,256]{3,2,1,0:T(8,128)} %refs_1_.1, f32[16,64,256]{2,1,0:T(8,128)} %refs_2_.1, f32[16,64,256]{2,1,0:T(8,128)} %refs_3_.1, f32[8,4,128,128]{3,2,1,0:T(8,128)} %refs_4_.1, ...), custom_call_target="tpu_custom_call" | custom-call | tf_op jit(solution)/shard_map/coupled/pallas_call | solution.py:567
  56.2 1.0 %copy.19 = f32[16,64,256]{2,1,0:T(8,128)} copy(f32[16,64,256]{2,1,0:T(8,128)S(1)} %get-tuple-element.9) | data formatting | bytes 2097152
  57.2 0.6 %copy.20 = f32[1024]{0:T(1024)} copy(f32[1024]{0:T(1024)S(1)} %bitcast.10) | data formatting | bytes 8192
  57.8 0.6 copy.21
